TPU v7x, 8 devices: a whole 2x2x1 slice. The times are simulated.
8 devices in a mesh: rep: 1 (over z), dp: 8 (over x, y, core).
Axes of the slice: x: 2, y: 2, z: 1, core: 2. Of those that a mesh axis runs over, the one named last changes fastest.
Arguments:
- x: bfloat16 [8, 2048, 1024], P(('rep', 'dp'))
- dy: bfloat16 [8, 2048, 1024], P(('rep', 'dp'))
- w_gate: bfloat16 [2, 1024, 2560], replicated
- w_up: bfloat16 [2, 1024, 2560], replicated
- w_down: bfloat16 [2, 2560, 1024], replicated
- m_w_gate: float32 [2, 1024, 2560], replicated
- m_w_up: float32 [2, 1024, 2560], replicated
- m_w_down: float32 [2, 2560, 1024], replicated
- v_w_gate: float32 [2, 1024, 2560], replicated
- v_w_up: float32 [2, 1024, 2560], replicated
- v_w_down: float32 [2, 2560, 1024], replicated
Outputs:
- output 1: bfloat16 [2, 1024, 2560], P('rep')
- output 2: bfloat16 [2, 1024, 2560], P('rep')
- output 3: bfloat16 [2, 2560, 1024], P('rep')
- output 4: float32 [2, 1024, 2560], P('rep')
- output 5: float32 [2, 1024, 2560], P('rep')
- output 6: float32 [2, 2560, 1024], P('rep')
- output 7: float32 [2, 1024, 2560], P('rep')
- output 8: float32 [2, 1024, 2560], P('rep')
- output 9: float32 [2, 2560, 1024], P('rep')
All inputs are finite; a program needn't handle non-finite values.
Results may differ from a plain program's by a relative error of at most 0.022.
Values are sent between devices in bfloat16 or wider.
A program may use at most 2.5 GiB of HBM per device.

v0:
```python
import jax
import jax.numpy as jnp
from jax import lax
from jax.sharding import PartitionSpec as P

NAMES = ("w_gate", "w_up", "w_down")


def matmul(a, w):
    return jnp.dot(a, w, preferred_element_type=jnp.float32).astype(jnp.bfloat16)


def normed(h):
    wide = h.astype(jnp.float32)
    scale = lax.rsqrt(jnp.mean(wide**2, -1, keepdims=True) + 1e-6)
    return (wide * scale).astype(jnp.bfloat16)


def layer(h, w):
    a = normed(h)
    gate = jnp.dot(a, w["w_gate"], preferred_element_type=jnp.float32)
    up = jnp.dot(a, w["w_up"], preferred_element_type=jnp.float32)
    return h + matmul((jax.nn.silu(gate) * up).astype(jnp.bfloat16), w["w_down"])


def adamw(w, m, v, g):
    m = 0.9 * m + 0.1 * g
    v = 0.95 * v + 0.05 * g * g
    step = m * lax.rsqrt(v + 1e-8) + 0.1 * w
    return (w - 0.02 * step).astype(jnp.bfloat16), m, v


def clipped(gradients, sum_of_squares, count):
    factor = jnp.minimum(1.0, 0.5 * lax.rsqrt(sum_of_squares / count + 1e-30))
    return [g * factor for g in gradients]


def solution(mesh):
    def step(x, dy, *arrays):
        weights, m, v = (arrays[i : i + 3] for i in (0, 3, 6))
        layers = weights[0].shape[0]
        h, kept = x[0], []
        for number in range(layers):
            kept.append(h)
            h = layer(h, {name: w[number] for name, w in zip(NAMES, weights, strict=True)})
        by_h, summed = dy[0], [None] * layers
        for number in reversed(range(layers)):
            _, back = jax.vjp(lambda w, h: layer(h, w), {name: w[number] for name, w in zip(NAMES, weights, strict=True)}, kept[number])
            by_w, by_h = back(by_h)
            summed[number] = [lax.psum(by_w[name], "dp") for name in NAMES]
        gradients = [jnp.stack([summed[number][i] for number in range(layers)]).astype(jnp.float32) for i in range(3)]
        gradients = clipped(gradients, sum(jnp.sum(g * g) for g in gradients), sum(g.size for g in gradients))
        new = [adamw(w.astype(jnp.float32), m, v, g) for w, m, v, g in zip(weights, m, v, gradients, strict=True)]
        return tuple(one[which] for which in range(3) for one in new)

    return jax.shard_map(
        step,
        mesh=mesh,
        in_specs=(P(("rep", "dp"), None, None),) * 2 + (P(None, None, None),) * 9,
        out_specs=(P("rep", None, None),) * 9,
        check_vma=False,
    )
```

profile of v0, /device:TPU:0, one launch (start us, length us, event | category | flops | bytes accessed | tf_op | source)
XLA Modules:
  0.0 837.5 jit_solution(7158035297244427637)
XLA Ops:
  7.2 6.5 copy.20
  16.8 6.7 copy.21
  23.5 16.9 %convolution_convert_fusion.1 = bf16[2048,2560]{1,0:T(8,128)(2,1)} fusion(bf16[2,2560,1024]{2,1,0:T(8,128)(2,1)} %param.15, bf16[1,2048,1024]{2,1,0:T(8,128)(2,1)} %param.12), kind=kOutput, calls=%fused_computation.63 | convolution fusion | flops 10742661120 | bytes 19922944 | tf_op jit(solution)/shard_map/transpose(jvp())/dot_general | solution.py:10
  40.4 14.1 %fusion.62 = f32[2048,2560]{1,0:T(8,128)} fusion(bf16[2,1024,2560]{2,1,0:T(8,128)(2,1)S(1)} %bitcast.77, bf16[1,2048,1024]{2,1,0:T(8,128)(2,1)S(1)} %copy-done.4, f32[2048]{0:T(1024)S(1)} %add_rsqrt_fusion), kind=kOutput, calls=%fused_computation.99 | convolution fusion | flops 10743709696 | bytes 30416896 | tf_op jit(solution)/shard_map/dot_general | solution.py:21
  54.5 26.7 %multiply_convert_fusion.1 = (bf16[2048,2560]{1,0:T(8,128)(2,1)}, f32[2048,2560]{1,0:T(8,128)}) fusion(f32[2048,2560]{1,0:T(8,128)} %fusion.62, bf16[2,1024,2560]{2,1,0:T(8,128)(2,1)} %param.14, bf16[1,2048,1024]{2,1,0:T(8,128)(2,1)} %param.11, f32[2048]{0:T(1024)S(1)} %add_rsqrt_fusion), kind=kOutput, calls=%fused_computation.53 | convolution fusion | flops 10775166976 | bytes 61874176 | tf_op jit(solution)/shard_map/dot_general | solution.py:22
  81.3 17.7 %fusion.40 = (f32[2048]{0:T(1024)S(1)}, bf16[2048,1024]{0,1:T(8,128)(2,1)}) fusion(bf16[2048,2560]{1,0:T(8,128)(2,1)} %get-tuple-element.24, bf16[2,2560,1024]{2,1,0:T(8,128)(2,1)} %param.15, bf16[1,2048,1024]{1,2,0:T(8,128)(2,1)S(1)} %copy-done.2), kind=kOutput, calls=%fused_computation.76 | convolution fusion | flops 10747901952 | bytes 24125440 | tf_op jit(solution)/shard_map/dot_general | solution.py:10
  98.9 18.5 %fusion.49 = f32[2048,2560]{1,0:T(8,128)} fusion(bf16[2,1024,2560]{2,1,0:T(8,128)(2,1)} %param.14, bf16[2048,1024]{0,1:T(8,128)(2,1)} %get-tuple-element.27, f32[2048]{0:T(1024)S(1)} %fusion.98), kind=kOutput, calls=%fused_computation.86 | convolution fusion | flops 10743709696 | bytes 30416896 | tf_op jit(solution)/shard_map/jvp()/dot_general | solution.py:22
  117.4 32.5 %fusion.20 = (bf16[2048,2560]{1,0:T(8,128)(2,1)}, f32[2048,2560]{1,0:T(8,128)}) fusion(f32[2048,2560]{1,0:T(8,128)} %fusion.49, bf16[2048,2560]{1,0:T(8,128)(2,1)} %convolution_convert_fusion.1, bf16[2,1024,2560]{2,1,0:T(8,128)(2,1)} %param.13, bf16[2048,1024]{0,1:T(8,128)(2,1)} %get-tuple-element.27, f32[2048]{0:T(1024)S(1)} %fusion.98), kind=kOutput, calls=%fused_computation.41 | convolution fusion | flops 10806624256 | bytes 72359936 | tf_op jit(solution)/shard_map/jvp()/dot_general | solution.py:21
  149.9 19.9 %fusion.33 = bf16[2048,1024]{0,1:T(8,128)(2,1)} fusion(bf16[2048,2560]{1,0:T(8,128)(2,1)} %convolution_convert_fusion.1, bf16[2,1024,2560]{2,1,0:T(8,128)(2,1)} %param.14, f32[2048,2560]{1,0:T(8,128)} %get-tuple-element.29), kind=kOutput, calls=%fused_computation.61 | convolution fusion | flops 10768875520 | bytes 40894464 | tf_op jit(solution)/shard_map/transpose(jvp())/dot_general | solution.py:22
  169.8 20.0 %fusion.71 = bf16[1,1024,2560]{2,1,0:T(8,128)(2,1)} fusion(bf16[2048,2560]{1,0:T(8,128)(2,1)} %convolution_convert_fusion.1, bf16[2048,1024]{0,1:T(8,128)(2,1)} %get-tuple-element.27, f32[2048]{0:T(1024)S(1)} %fusion.98, f32[2048,2560]{1,0:T(8,128)} %get-tuple-element.29), kind=kOutput, calls=%fused_computation.106 | convolution fusion | flops 10777788416 | bytes 40902656 | tf_op jit(solution)/shard_map/transpose(jvp())/dot_general | solution.py:22
  189.8 22.1 %fusion.72 = bf16[1,2560,1024]{2,1,0:T(8,128)(2,1)} fusion(f32[2048,2560]{1,0:T(8,128)} %fusion.49, bf16[1,2048,1024]{2,1,0:T(8,128)(2,1)} %param.12, f32[2048,2560]{1,0:T(8,128)} %get-tuple-element.29), kind=kOutput, calls=%fused_computation.107 | convolution fusion | flops 10771496960 | bytes 51380224 | tf_op jit(solution)/shard_map/transpose(jvp())/dot_general | solution.py:10
  211.9 16.6 %fusion.73 = bf16[1,1024,2560]{2,1,0:T(8,128)(2,1)} fusion(bf16[2048,2560]{1,0:T(8,128)(2,1)} %get-tuple-element.28, bf16[2048,1024]{0,1:T(8,128)(2,1)} %get-tuple-element.27, f32[2048]{0:T(1024)S(1)} %fusion.98), kind=kOutput, calls=%fused_computation.108 | convolution fusion | flops 10743709696 | bytes 19931136 | tf_op jit(solution)/shard_map/transpose(jvp())/dot_general | solution.py:21
  228.5 16.8 %fusion.42 = (f32[2048]{0:T(1024)S(1)}, bf16[2048,1024]{0,1:T(8,128)(2,1)S(1)}) fusion(bf16[2048,1024]{0,1:T(8,128)(2,1)S(1)} %copy-done.3, bf16[2048,1024]{0,1:T(8,128)(2,1)} %fusion.33, bf16[2048,2560]{1,0:T(8,128)(2,1)} %get-tuple-element.28, bf16[2,1024,2560]{2,1,0:T(8,128)(2,1)} %param.13), kind=kOutput, calls=%fused_computation.78 | convolution fusion | flops 10747901952 | bytes 28319744 | tf_op jit(solution)/shard_map/transpose(jvp())/dot_general | solution.py:21
  245.4 3.2 fusion.82
  248.5 15.8 %convolution_convert_fusion = bf16[2048,2560]{1,0:T(8,128)(2,1)} fusion(bf16[2048,1024]{0,1:T(8,128)(2,1)S(1)} %fusion.82, bf16[2,2560,1024]{2,1,0:T(8,128)(2,1)} %param.15), kind=kOutput, calls=%fused_computation.62 | convolution fusion | flops 10742661120 | bytes 19922944 | tf_op jit(solution)/shard_map/transpose(jvp())/dot_general | solution.py:10
  264.4 15.6 %fusion.74 = bf16[1,2560,1024]{2,1,0:T(8,128)(2,1)} fusion(bf16[2048,2560]{1,0:T(8,128)(2,1)} %get-tuple-element.24, bf16[2048,1024]{0,1:T(8,128)(2,1)S(1)} %fusion.82), kind=kOutput, calls=%fused_computation.109 | convolution fusion | flops 10740039680 | bytes 19922944 | tf_op jit(solution)/shard_map/transpose(jvp())/dot_general | solution.py:10
  280.0 20.0 %fusion.67 = bf16[1,1024,2560]{2,1,0:T(8,128)(2,1)} fusion(bf16[2048,2560]{1,0:T(8,128)(2,1)} %convolution_convert_fusion, bf16[1,2048,1024]{1,2,0:T(8,128)(2,1)} %copy.20, f32[2048]{0:T(1024)S(1)} %copy-done.8, f32[2048,2560]{1,0:T(8,128)} %fusion.62), kind=kOutput, calls=%fused_computation.104 | convolution fusion | flops 10777788416 | bytes 40902656 | tf_op jit(solution)/shard_map/transpose(jvp())/dot_general | solution.py:22
  299.9 25.0 %fusion.68 = bf16[1,1024,2560]{2,1,0:T(8,128)(2,1)} fusion(f32[2048,2560]{1,0:T(8,128)} %fusion.62, f32[2048,2560]{1,0:T(8,128)} %get-tuple-element.25, bf16[2048,2560]{1,0:T(8,128)(2,1)} %convolution_convert_fusion, bf16[1,2048,1024]{1,2,0:T(8,128)(2,1)} %copy.20, f32[2048]{0:T(1024)S(1)} %copy-done.8), kind=kOutput, calls=%fused_computation.105 | convolution fusion | flops 10804002816 | bytes 61874176 | tf_op jit(solution)/shard_map/transpose(jvp())/dot_general | solution.py:21
  324.9 366.3 %all-reduce.3.cloned.1.call-done = (bf16[1,1024,2560]{2,1,0:T(8,128)(2,1)}, bf16[1,1024,2560]{2,1,0:T(8,128)(2,1)}, bf16[1,1024,2560]{2,1,0:T(8,128)(2,1)}, bf16...) async-done(((bf16[1,1024,2560]{2,1,0:T(8,128)(2,1)}, bf16[1,1024,2560]{2,1,0:T(8,128)(2,1)}, ...) | async-done | bytes 31457296 | tf_op jit(solution)/shard_map/psum | solution.py:50
  691.2 9.4 %fusion.10 = f32[]{:T(128)} fusion(bf16[1,1024,2560]{2,1,0:T(8,128)(2,1)} %get-tuple-element.9, bf16[1,1024,2560]{2,1,0:T(8,128)(2,1)} %get-tuple-element.10), kind=kLoop, calls=%fused_computation.31 | loop fusion | flops 20971520 | bytes 10485764 | tf_op jit(solution)/shard_map/reduce_sum | solution.py:52
  700.7 6.0 fusion.11
  708.0 8.5 %fusion.12 = f32[]{:T(128)} fusion(bf16[1,2560,1024]{2,1,0:T(8,128)(2,1)} %get-tuple-element.13, bf16[1,2560,1024]{2,1,0:T(8,128)(2,1)} %get-tuple-element.14), kind=kLoop, calls=%fused_computation.33 | loop fusion | flops 20971520 | bytes 10485764 | tf_op jit(solution)/shard_map/reduce_sum | solution.py:52
  717.2 40.1 %fusion.18 = (bf16[2,2560,1024]{2,1,0:T(8,128)(2,1)}, f32[2,2560,1024]{2,1,0:T(8,128)}, f32[2,2560,1024]{2,1,0:T(8,128)}) fusion(bf16[2,2560,1024]{2,1,0:T(8,128)(2,1)} %param.15, f32[]{:T(128)S(6)} %min_shard_map.3, bf16[1,2560,1024]{2,1,0:T(8,128)(2,1)} %get-tuple-element.13, bf16[1,2560,1024]{2,1,0:T(8,128)(2,1)} %get-tuple-element.14, ...), kind=kLoop, calls=%fused_computation.39 | loop fusion | flops 104857600 | bytes 115343360 | tf_op jit(solution)/shard_map/convert_element_type | solution.py:30
  757.4 72.8 %fusion.8 = (bf16[2,1024,2560]{2,1,0:T(8,128)(2,1)}, f32[2,1024,2560]{2,1,0:T(8,128)}, f32[2,1024,2560]{2,1,0:T(8,128)}, bf16[2,1024,2560]{2,1,0:T(8,128)(2,1)},...) fusion(bf16[2,1024,2560]{2,1,0:T(8,128)(2,1)} %param.13, f32[]{:T(128)S(6)} %min_shard_map.3, ...), kind=kLoop, calls=%fused_computation.29 | loop fusion | flops 209715200 | bytes 230686720 | tf_op jit(solution)/shard_map/convert_element_type | solution.py:30
  (36 shorter events, 3.2 us)
Async XLA Ops:
  7.2 684.1 %all-reduce.3.cloned.1.call-start = ((), (), s32[]{:S(2)}) async-start(), calls=%async_computation | async-start | bytes 62914560 | tf_op jit(solution)/shard_map/psum | solution.py:50
  16.8 37.7 %copy-start.7 = (f32[2048]{0:T(1024)}, f32[2048]{0:T(1024)S(1)}, u32[]{:S(2)}) copy-start(f32[2048]{0:T(1024)S(1)} %add_rsqrt_fusion) | copy-start | bytes 24580
  16.8 23.6 %slice-start.2 = ((s8[10485760]{0:T(1024)(128)(4,1)}), s8[2097152]{0:T(1024)(128)(4,1)S(1)}, s32[]{:S(2)}) async-start(s8[10485760]{0:T(1024)(128)(4,1)} %bitcast.76), calls=%async_computation.3 | async-start | bytes 4194304
  23.5 16.9 %slice-start.3 = ((s8[10485760]{0:T(1024)(128)(4,1)}), s8[4194304]{0:T(1024)(128)(4,1)S(1)}, s32[]{:S(2)}) async-start(s8[10485760]{0:T(1024)(128)(4,1)} %bitcast.76), calls=%async_computation.4 | async-start | bytes 8388608
  23.5 16.9 %slice-start.4 = ((s8[10485760]{0:T(1024)(128)(4,1)}), s8[4194304]{0:T(1024)(128)(4,1)S(1)}, s32[]{:S(2)}) async-start(s8[10485760]{0:T(1024)(128)(4,1)} %bitcast.76), calls=%async_computation.5 | async-start | bytes 8388608
  23.5 16.9 %copy-start.4 = (bf16[1,2048,1024]{2,1,0:T(8,128)(2,1)S(1)}, bf16[1,2048,1024]{2,1,0:T(8,128)(2,1)}, u32[]{:S(2)}) copy-start(bf16[1,2048,1024]{2,1,0:T(8,128)(2,1)} %param.11) | copy-start | bytes 12582916
  54.5 26.7 %copy-start.2 = (bf16[1,2048,1024]{1,2,0:T(8,128)(2,1)S(1)}, bf16[1,2048,1024]{1,2,0:T(8,128)(2,1)}, u32[]{:S(2)}) copy-start(bf16[1,2048,1024]{1,2,0:T(8,128)(2,1)} %copy.20) | copy-start | bytes 12582916
  98.9 18.5 %copy-start.5 = (f32[2048]{0:T(1024)}, f32[2048]{0:T(1024)S(1)}, u32[]{:S(2)}) copy-start(f32[2048]{0:T(1024)S(1)} %get-tuple-element.26) | copy-start | bytes 24580
  211.9 16.6 %copy-start.3 = (bf16[2048,1024]{0,1:T(8,128)(2,1)S(1)}, bf16[2048,1024]{0,1:T(8,128)(2,1)}, u32[]{:S(2)}) copy-start(bf16[2048,1024]{0,1:T(8,128)(2,1)} %get-tuple-element.27) | copy-start | bytes 12582916
  228.5 16.8 %copy-start.6 = (f32[2048]{0:T(1024)S(1)}, f32[2048]{0:T(1024)}, u32[]{:S(2)}) copy-start(f32[2048]{0:T(1024)} %copy-done.5) | copy-start | bytes 24580
  228.5 16.9 %copy-start.1 = (bf16[1,2048,1024]{1,2,0:T(8,128)(2,1)S(1)}, bf16[1,2048,1024]{1,2,0:T(8,128)(2,1)}, u32[]{:S(2)}) copy-start(bf16[1,2048,1024]{1,2,0:T(8,128)(2,1)} %copy.21) | copy-start | bytes 12582916
  264.4 15.6 %copy-start.8 = (f32[2048]{0:T(1024)S(1)}, f32[2048]{0:T(1024)}, u32[]{:S(2)}) copy-start(f32[2048]{0:T(1024)} %copy-done.7) | copy-start | bytes 24580
  691.2 9.5 %slice-start = ((s8[5242880]{0:T(1024)(128)(4,1)}), s8[4194304]{0:T(1024)(128)(4,1)S(1)}, s32[]{:S(2)}) async-start(s8[5242880]{0:T(1024)(128)(4,1)} %bitcast.74), calls=%async_computation.1 | async-start | bytes 8388608
  691.2 9.5 %copy-start = (bf16[1,1024,2560]{2,1,0:T(8,128)(2,1)S(1)}, bf16[1,1024,2560]{2,1,0:T(8,128)(2,1)}, u32[]{:S(2)}) copy-start(bf16[1,1024,2560]{2,1,0:T(8,128)(2,1)} %get-tuple-element.12) | copy-start | bytes 15728644
  691.2 9.5 %slice-start.1 = ((s8[5242880]{0:T(1024)(128)(4,1)}), s8[1048576]{0:T(1024)(128)(4,1)S(1)}, s32[]{:S(2)}) async-start(s8[5242880]{0:T(1024)(128)(4,1)} %bitcast.74), calls=%async_computation.2 | async-start | bytes 2097152
Sparse Core Ops, SparseCore 0:
  325.0 366.1 all-reduce.2
where the time goes:
time: 846 us; the launch traced here: 837 us
  waiting for transfers between devices  366 us (43%)
  matrix products  298 us (35%)
  other arithmetic  143 us (17%)
  between operations  16.6 us (2%)
  local copies, waits for them, and re-layouts  13.2 us (2%)
    psum x1, waiting for transfers between devices, step(): summed[number] = [lax.psum(by_w[name], 'dp') for name in NAMES]  366 us
    convert_element_type x2, other arithmetic, adamw(): return ((w - 0.02 * step).astype(jnp.bfloat16), m, v)  113 us
    dot_general x5, matrix products, layer(): up = jnp.dot(a, w['w_up'], preferred_element_type=jnp.float32)  105 us
    dot_general x5, matrix products, layer(): gate = jnp.dot(a, w['w_gate'], preferred_element_type=jnp.float32)  105 us
    dot_general x5, matrix products, matmul(): jnp.dot(a, w, preferred_element_type=jnp.float32).astype(jnp.bfloat16)  88.1 us
    reduce_sum x3, other arithmetic, step(): jnp.sum(g * g)  24 us
  transfers between devices with their start and end apart: 1, of which 1 were waited for; matrix products, arithmetic and copies ran while one was open for 0% of the time, Pallas kernels for 0%

commit v1 on v0

v1 whole, which is shorter than its diff:
```python
import jax
import jax.numpy as jnp
from jax import lax
from jax.experimental import pallas as pl
from jax.experimental.pallas import tpu as pltpu
from jax.sharding import PartitionSpec as P


T, D, F, L = 2048, 1024, 2560, 2
FT = 256
BLK = 128
SUB = 512
HALVES = (0, F // 2)
WIDE = F // 2
F32, BF16 = jnp.float32, jnp.bfloat16
MB = 1 << 20

NT = (((1,), (1,)), ((), ()))


def dot(a, b):
    return jnp.dot(a, b, preferred_element_type=F32)


def dot_nt(a, b):
    return lax.dot_general(a, b, NT, preferred_element_type=F32)


def sigmoid(x):
    return 0.5 * jnp.tanh(0.5 * x) + 0.5


def normed(h):
    wide = h.astype(F32)
    scale = lax.rsqrt(jnp.mean(wide * wide, -1, keepdims=True) + 1e-6)
    return (wide * scale).astype(BF16)


def place(shard, me):
    s = shard ^ me
    sx, sy, half = (s >> 2) & 1, (s >> 1) & 1, s & 1
    core = shard & 1
    return half * 4 + (1 - core) * (sx * 2 + sy) + core * (sy * 2 + sx)


def shard_at(p, me):
    half, k = p >> 2, p & 3
    hi, lo = k >> 1, k & 1
    core = (me & 1) ^ half
    sx, sy = (1 - core) * hi + core * lo, (1 - core) * lo + core * hi
    return me ^ (sx * 4 + sy * 2 + half)


def store_turned(me, tile, out_ref):
    for shard in range(8):
        rows = pl.ds(pl.multiple_of(place(jnp.int32(shard), me) * BLK, BLK), BLK)
        out_ref[rows, :] = tile[:, shard * BLK : (shard + 1) * BLK].T


def call(kernel, grid, ins, outs, scratch=(), flops=0, moved=0, aliases=None):
    return pl.pallas_call(
        kernel,
        grid_spec=pltpu.PrefetchScalarGridSpec(num_scalar_prefetch=1, grid=grid, in_specs=[s for s in ins], out_specs=[s for s, _ in outs], scratch_shapes=list(scratch)),
        out_shape=[o for _, o in outs],
        compiler_params=pltpu.CompilerParams(dimension_semantics=("arbitrary",) * len(grid), vmem_limit_bytes=63 * MB),
        cost_estimate=pl.CostEstimate(flops=int(flops), bytes_accessed=int(moved), transcendentals=0),
        input_output_aliases=aliases or {},
    )


def shaped(shape, dtype=BF16):
    return jax.ShapeDtypeStruct(shape, dtype)


MM = 2 * T * D * F


def prep(me, x, dy):
    rows = 256

    def kernel(me_ref, x_ref, dy_ref, a_ref, at_ref, dyt_ref):
        a = normed(x_ref[...])
        a_ref[...] = a
        store_turned(me_ref[0], a, at_ref)
        store_turned(me_ref[0], dy_ref[...], dyt_ref)

    tall = pl.BlockSpec((rows, D), lambda i, m: (i, 0))
    wide = pl.BlockSpec((D, rows), lambda i, m: (0, i))
    return call(kernel, (T // rows,), [tall, tall], [(tall, shaped((T, D))), (wide, shaped((D, T))), (wide, shaped((D, T)))], flops=MM // 3, moved=20e6)(me, x, dy)


def gate_up(me, a, w_gate, w_up):
    def kernel(me_ref, a_ref, wg_ref, wu_ref, g_ref, u_ref, act_ref):
        for t in range(T // SUB):
            rows = slice(t * SUB, (t + 1) * SUB)
            g = dot(a_ref[rows], wg_ref[0])
            u = dot(a_ref[rows], wu_ref[0])
            g_ref[rows, :] = g
            u_ref[rows, :] = u
            act_ref[rows, :] = (g * sigmoid(g) * u).astype(BF16)

    weight = pl.BlockSpec((1, D, FT), lambda j, m: (0, 0, j))
    tile = pl.BlockSpec((T, FT), lambda j, m: (0, j))
    return call(
        kernel,
        (F // FT,),
        [pl.BlockSpec((T, D), lambda j, m: (0, 0)), weight, weight],
        [(tile, shaped((T, F), F32)), (tile, shaped((T, F), F32)), (tile, shaped((T, F)))],
        flops=2 * MM,
        moved=67e6,
    )(me, a, w_gate, w_up)


def down(me, act, w_down, h):
    rows = 512

    def kernel(me_ref, act_ref, wd_ref, h_ref, out_ref, a_ref, at_ref):
        out = h_ref[...] + dot(act_ref[...], wd_ref[0]).astype(BF16)
        out_ref[...] = out
        a = normed(out)
        a_ref[...] = a
        store_turned(me_ref[0], a, at_ref)

    tall = pl.BlockSpec((rows, D), lambda i, m: (i, 0))
    return call(
        kernel,
        (T // rows,),
        [pl.BlockSpec((rows, F), lambda i, m: (i, 0)), pl.BlockSpec((1, F, D), lambda i, m: (0, 0, 0), pipeline_mode=pl.Buffered(1)), tall],
        [(tall, shaped((T, D))), (tall, shaped((T, D))), (pl.BlockSpec((D, rows), lambda i, m: (0, i)), shaped((D, T)))],
        flops=MM,
        moved=32e6,
    )(me, act, w_down, h)


def both(a, b):
    return (a.astype(F32) + b.astype(F32)).astype(BF16)


def grads(layer, a, at, dh, dht, w_gate, w_up, w_down, kept=None):
    make = kept is None
    n = F // FT

    def kernel(*refs):
        refs = list(refs)
        take = lambda count: [refs.pop(0) for _ in range(count)]
        hbm = take(4 if make else 3)
        (wd_ref,) = take(1)
        one, two = take(2)
        own_ref, sq_ref = take(2)
        dg_ref, du_ref = take(2)
        (act_ref,) = take(1)
        mine = take(len(hbm))
        keep, send, recv0, away1, stay1, recv1, away2, stay2, recv2 = take(9)
        sems, s0, r0, s1, r1, s2, r2 = take(7)
        copies = [pltpu.make_async_copy(s, d, sems.at[i]) for i, (s, d) in enumerate(zip(hbm, mine))]
        if make:
            dh_v, a_v, at_v, dht_v = mine
        else:
            dh_v, at_v, dht_v = mine
        early = 2 if make else 1
        j = pl.program_id(0)
        me = lax.axis_index("dp")
        core = me % 2
        other = me + 1 - 2 * core
        xs, ys = me + 4 - 8 * (me // 4), me + 2 - 4 * ((me // 2) % 2)
        near, far = (1 - core) * xs + core * ys, (1 - core) * ys + core * xs

        def remote(src, dst, ss, rs, to):
            return pltpu.make_async_remote_copy(src, dst, ss, rs, device_id={"dp": to}, device_id_type=pl.DeviceIdType.MESH)

        def core_copy(t):
            return remote(send.at[t % 2], recv0.at[t % 2], s0.at[t % 2], r0.at[t % 2], other)

        def near_copy(t):
            return remote(away1.at[t % 2], recv1.at[t % 4], s1.at[t % 2], r1.at[t % 4], near)

        def far_copy(t):
            return remote(away2.at[t % 2], recv2.at[t % 4], s2.at[t % 2], r2.at[t % 4], far)

        barrier = pltpu.get_barrier_semaphore()

        @pl.when(j == 0)
        def _():
            for to in (other, xs, ys):
                pl.semaphore_signal(barrier, inc=1, device_id={"dp": to}, device_id_type=pl.DeviceIdType.MESH)
            for c in copies:
                c.start()
            sq_ref[...] = jnp.zeros_like(sq_ref)

        @pl.when(j >= 6)
        def _():
            t = j - 6
            far_copy(t).wait()
            for i in range(3):
                done = both(stay2[t % 2, i], recv2[t % 4, i])
                own_ref[i] = done
                done = done.astype(F32)
                done = jnp.sum((done * done).reshape(BLK // 8, 8, FT), 0)
                sq_ref[...] += done[:, :128] + done[:, 128:]

        @pl.when((j >= 4) & (j < n + 4))
        def _():
            t = j - 4
            near_copy(t).wait()
            for i in range(3):
                away2[t % 2, i] = both(stay1[t % 2, 1, i], recv1[t % 4, 1, i])
                stay2[t % 2, i] = both(stay1[t % 2, 0, i], recv1[t % 4, 0, i])

        @pl.when((j >= 2) & (j < n + 2))
        def _():
            t = j - 2
            core_copy(t).wait()
            for k in range(2):
                for i in range(3):
                    away1[t % 2, k, i] = both(keep[t % 2, 2 + k, i], recv0[t % 2, 2 + k, i])
                    stay1[t % 2, k, i] = both(keep[t % 2, k, i], recv0[t % 2, k, i])

        def tokens(t):
            rows = slice(t * SUB, (t + 1) * SUB)
            if make:
                g, u = dot(a_v[rows], one[0]), dot(a_v[rows], two[0])
            else:
                g, u = one[rows, :], two[rows, :]
            dact = dot_nt(dh_v[rows], wd_ref[0]).astype(BF16).astype(F32)
            s = sigmoid(g)
            gs = g * s
            act_ref[rows, :] = (gs * u).astype(BF16)
            du_ref[rows, :] = (dact * gs).astype(BF16)
            dg_ref[rows, :] = (dact * u * (s + gs * (1.0 - s))).astype(BF16)

        @pl.when(j == 0)
        def _():
            for c in copies[:early]:
                c.wait()

        @pl.when(j < n)
        def _():
            tokens(0)

        @pl.when(j == 0)
        def _():
            pl.semaphore_wait(barrier, 3)

        @pl.when((j >= 4) & (j < n + 4))
        def _():
            far_copy(j - 4).start()

        @pl.when((j >= 2) & (j < n + 2))
        def _():
            near_copy(j - 2).start()

        @pl.when((j >= 1) & (j < n + 1))
        def _():
            core_copy(j - 1).start()

        @pl.when(j < n)
        def _():
            for t in range(1, T // SUB):
                tokens(t)

        @pl.when(j == 0)
        def _():
            for c in copies[early:]:
                c.wait()

        @pl.when(j < n)
        def _():
            for i, (left, right) in enumerate(((at_v, dg_ref), (at_v, du_ref), (dht_v, act_ref))):
                for half, out in enumerate((keep, send)):
                    made = dot(left[half * 4 * BLK : (half + 1) * 4 * BLK, :], right[...]).astype(BF16)
                    for k in range(4):
                        out[j % 2, k, i] = made[k * BLK : (k + 1) * BLK]

    last = n - 1
    whole = pl.BlockSpec(memory_space=pl.ANY)
    weight = pl.BlockSpec((1, D, FT), lambda j: (layer, 0, jnp.minimum(j, last)))
    wdown = pl.BlockSpec((1, FT, D), lambda j: (layer, jnp.minimum(j, last), 0))
    tile = pl.BlockSpec((T, FT), lambda j: (0, jnp.minimum(j, last)))
    outs = [
        (pl.BlockSpec((3, BLK, FT), lambda j: (0, 0, jnp.clip(j - 6, 0, last))), shaped((3, BLK, F))),
        (pl.BlockSpec((8, 128), lambda j: (0, 0)), shaped((8, 128), F32)),
    ]
    temp = pltpu.VMEM((T, FT), BF16)
    if make:
        args = [dh, a, at, dht, w_down, w_gate, w_up]
        ins = [whole] * 4 + [wdown, weight, weight]
        outs += [(tile, shaped((T, F)))] * 2
        scratch = [temp] + [pltpu.VMEM((T, D), BF16)] * 2 + [pltpu.VMEM((D, T), BF16)] * 2
    else:
        args = [dh, at, dht, w_down, *kept]
        ins = [whole] * 3 + [wdown, tile, tile]
        scratch = [temp] * 3 + [pltpu.VMEM((T, D), BF16)] + [pltpu.VMEM((D, T), BF16)] * 2
    quarter = lambda *lead: pltpu.VMEM((*lead, 3, BLK, FT), BF16)
    scratch += [quarter(2, 4), quarter(2, 4), quarter(2, 4), quarter(2, 2), quarter(2, 2), quarter(4, 2), quarter(2), quarter(2), quarter(4)]
    sem = pltpu.SemaphoreType.DMA
    scratch += [sem((4 if make else 3,)), sem((2,)), sem((2,)), sem((2,)), sem((4,)), sem((2,)), sem((4,))]
    return pl.pallas_call(
        kernel,
        grid_spec=pltpu.PrefetchScalarGridSpec(num_scalar_prefetch=0, grid=(n + 6,), in_specs=ins, out_specs=[s for s, _ in outs], scratch_shapes=scratch),
        out_shape=[o for _, o in outs],
        compiler_params=pltpu.CompilerParams(
            dimension_semantics=("arbitrary",), vmem_limit_bytes=63 * MB, collective_id=layer, has_side_effects=True
        ),
        cost_estimate=pl.CostEstimate(flops=(6 if make else 4) * MM, bytes_accessed=60_000_000, transcendentals=0),
    )(*args)


def back(me, dg, du, w_gate, w_up, h, dh):
    rows = 512

    def kernel(me_ref, dg_ref, du_ref, wg_ref, wu_ref, h_ref, dh_ref, out_ref, outt_ref):
        da = (dot_nt(dg_ref[...], wg_ref[0]) + dot_nt(du_ref[...], wu_ref[0])).astype(BF16).astype(F32)
        wide = h_ref[...].astype(F32)
        scale = lax.rsqrt(jnp.mean(wide * wide, -1, keepdims=True) + 1e-6)
        along = jnp.mean(da * wide, -1, keepdims=True) * (scale * scale * scale)
        out = dh_ref[...] + (da * scale - wide * along).astype(BF16)
        out_ref[...] = out
        store_turned(me_ref[0], out, outt_ref)

    tall = pl.BlockSpec((rows, D), lambda i, m: (i, 0))
    broad = pl.BlockSpec((rows, F), lambda i, m: (i, 0))
    weight = pl.BlockSpec((1, D, F), lambda i, m: (1, 0, 0), pipeline_mode=pl.Buffered(1))
    return call(
        kernel,
        (T // rows,),
        [broad, broad, weight, weight, tall, tall],
        [(tall, shaped((T, D))), (pl.BlockSpec((D, rows), lambda i, m: (0, i)), shaped((D, T)))],
        flops=2 * MM,
        moved=48e6,
    )(me, dg, du, w_gate, w_up, h, dh)


def adamw(me, layer, first, factor, parts, w, m, v, so_far):
    ft = 640
    steps, at0 = WIDE // ft, first // ft

    def kernel(me_ref, f_ref, *refs):
        parts, refs = refs[:8], refs[8:]
        ws, ms, vs = refs[0:3], refs[3:6], refs[6:9]
        nws, nms, nvs, part = refs[-10:-7], refs[-7:-4], refs[-4:-1], refs[-1]
        f = f_ref[0, 0]
        p = pl.program_id(0)
        for at in range(8):

            @pl.when(p == at)
            def _(at=at):
                part[...] = parts[at][...]

        def take(i, rows, g):
            g = g.astype(F32) * f
            new_m = 0.9 * ms[i][0, rows, :] + 0.1 * g
            new_v = 0.95 * vs[i][0, rows, :] + 0.05 * g * g
            wide = ws[i][0, rows, :].astype(F32)
            nws[i][0, rows, :] = (wide - 0.02 * (new_m * lax.rsqrt(new_v + 1e-8) + 0.1 * wide)).astype(BF16)
            nms[i][0, rows, :] = new_m
            nvs[i][0, rows, :] = new_v

        for r in range(0, BLK, 16):
            for i in range(2):
                take(i, slice(r, r + 16), part[i, r : r + 16, :])
        for r in range(0, ft, 128):
            take(2, slice(r, r + 128), part[2, :, r : r + 128].T)

    def piece(at):
        return pl.BlockSpec((3, BLK, ft), lambda p, j, me_ref: (0, 0, jnp.where(p == at, j, jnp.where(p < at, 0, steps - 1))))

    across = pl.BlockSpec((1, BLK, ft), lambda p, j, me_ref: (layer, shard_at(p, me_ref[0]), at0 + j))
    along = pl.BlockSpec((1, ft, BLK), lambda p, j, me_ref: (layer, at0 + j, shard_at(p, me_ref[0])))
    three = [across, across, along]
    whole = pl.BlockSpec(memory_space=pl.ANY)
    ins = [pl.BlockSpec(memory_space=pltpu.SMEM)] + [piece(at) for at in range(8)] + three * 3
    args = [factor] + list(parts) + list(w) + list(m) + list(v)
    outs = [(s, shaped(o.shape, o.dtype)) for s, o in zip(three * 3, list(w) + list(m) + list(v))]
    aliases = {}
    if so_far is not None:
        aliases = {1 + len(ins) + i: i for i in range(9)}
        ins, args = ins + [whole] * 9, args + list(so_far)
    size = 3 * WIDE * D
    return call(kernel, (8, steps), ins, outs, [pltpu.VMEM((3, BLK, ft), BF16)], flops=size * 200, moved=size * 22, aliases=aliases)(me, *args)


CORE = [(i, i ^ 1) for i in range(8)]
FIRST = [(i, i ^ (2 if i & 1 else 4)) for i in range(8)]
SECOND = [(i, i ^ (4 if i & 1 else 2)) for i in range(8)]


STAGES = {"core": CORE, "first": FIRST, "second": SECOND}


def swap(a, stage):
    return lax.ppermute(a, "dp", STAGES[stage])


def gather(own):
    mine = [own, swap(own, "second")]
    mine += [swap(a, "first") for a in mine]
    return mine + [swap(a, "core") for a in mine]


def solution(mesh):
    def work(x, dy, *arrays):
        weights, m, v = (arrays[i : i + 3] for i in (0, 3, 6))
        w_gate, w_up, w_down = weights
        x, dy = x[0], dy[0]
        me = lax.axis_index("dp").astype(jnp.int32).reshape(1)
        a0, a0t, dyt = prep(me, x, dy)
        gate, up, act = gate_up(me, a0, w_gate, w_up)
        h, a1, a1t = down(me, act, w_down, x)

        own1, squares1, dg, du = grads(1, a1, a1t, dy, dyt, *weights)
        dh, dht = back(me, dg, du, w_gate, w_up, h, dy)
        own0, squares0 = grads(0, a0, a0t, dh, dht, *weights, kept=(gate, up))

        squares = lax.psum(jnp.sum(squares1 + squares0), "dp")
        factor = jnp.minimum(1.0, 0.5 * lax.rsqrt(squares / (3 * L * D * F) + 1e-30)).reshape(1, 1)

        new = None
        for layer, own in ((1, own1), (0, own0)):
            for first in HALVES:
                parts = gather(own[:, :, first : first + WIDE])
                new = adamw(me, layer, first, factor, parts, weights, m, v, new)
        return tuple(new)

    return jax.shard_map(
        work,
        mesh=mesh,
        in_specs=(P(("rep", "dp"), None, None),) * 2 + (P(None, None, None),) * 9,
        out_specs=(P("rep", None, None),) * 9,
        check_vma=False,
    )
```

time: 846 us -> 541 us (0.64)
  Pallas kernels: 0 us -> 415 us
  matrix products: 298 us -> 0 us
  waiting for transfers between devices: 366 us -> 73.9 us
  other arithmetic: 143 us -> 1.28 us
  blocking collectives: 0 us -> 23.3 us
  starting transfers between devices: 0.04 us -> 17.6 us
  between operations: 16.6 us -> 1.7 us
    pallas_call x0 -> x10, Pallas kernels: none -> 415 us  [the longest x2 195 us: grads(): pl.pallas_call(kernel, grid_spec=pltpu.PrefetchScalarGridSpec(num_scalar_...]
    psum x1 -> x0, waiting for transfers between devices: 366 us -> none  [step(): summed[number] = [lax.psum(by_w[name], 'dp') for name in NAMES]]
    dot_general x15 -> x0, matrix products: 298 us -> none  [the longest x5 105 us: layer(): up = jnp.dot(a, w['w_up'], preferred_element_type=jnp.float32)]
    convert_element_type x2 -> x0, other arithmetic: 113 us -> none  [adamw(): return ((w - 0.02 * step).astype(jnp.bfloat16), m, v)]
    ppermute x0 -> x28, waiting for transfers between devices: none -> 73.9 us  [swap(): return lax.ppermute(a, 'dp', STAGES[stage])]
    reduce_sum x4 -> x1, other arithmetic: 27 us -> 1.28 us  [work(): squares = lax.psum(jnp.sum(squares1 + squares0), 'dp')]
    psum x0 -> x1, blocking collectives: none -> 23.3 us  [work(): squares = lax.psum(jnp.sum(squares1 + squares0), 'dp')]
    ppermute x0 -> x28, starting transfers between devices: none -> 17.6 us  [swap(): return lax.ppermute(a, 'dp', STAGES[stage])]
  transfers between devices with their start and end apart: 1 -> 28, of which waited for: 1 -> 7; matrix products, arithmetic and copies ran while one was open for 0% -> 1% of each run, Pallas kernels for 0% -> 40%
where the time goes in v1:
time: 541 us; the launch traced here: 540 us
  Pallas kernels  415 us (77%)
  waiting for transfers between devices  73.9 us (14%)
  blocking collectives  23.3 us (4%)
  starting transfers between devices  17.6 us (3%)
  local copies, waits for them, and re-layouts  6.9 us (1%)
    pallas_call x2, Pallas kernels, grads(): pl.pallas_call(kernel, grid_spec=pltpu.PrefetchScalarGridSpec(num_scalar_...  195 us
    pallas_call x4, Pallas kernels, adamw(): call(kernel, (8, steps), ins, outs, [pltpu.VMEM((3, BLK, ft), BF16)], flo...  128 us
    ppermute x28, waiting for transfers between devices, swap(): return lax.ppermute(a, 'dp', STAGES[stage])  73.9 us
    pallas_call x1, Pallas kernels, back(): call(kernel, (T // rows,), [broad, broad, weight, weight, tall, tall], [(...  33.1 us
    pallas_call x1, Pallas kernels, gate_up(): call(kernel, (F // FT,), [pl.BlockSpec((T, D), lambda j, m: (0, 0)), weig...  28.6 us
    psum x1, blocking collectives, work(): squares = lax.psum(jnp.sum(squares1 + squares0), 'dp')  23.3 us
    pallas_call x1, Pallas kernels, down(): call(kernel, (T // rows,), [pl.BlockSpec((rows, F), lambda i, m: (i, 0)),...  19.7 us
    ppermute x28, starting transfers between devices, swap(): return lax.ppermute(a, 'dp', STAGES[stage])  17.6 us
  transfers between devices with their start and end apart: 28, of which 7 were waited for; matrix products, arithmetic and copies ran while one was open for 1% of the time, Pallas kernels for 40%

profile of v1, /device:TPU:0, one launch (start us, length us, event | category | flops | bytes accessed | tf_op | source)
XLA Modules:
  0.0 539.8 jit_solution(12089127797915807629)
XLA Ops:
  0.6 11.0 %shard_map.178 = (bf16[2048,1024]{1,0:T(8,128)(2,1)}, bf16[1024,2048]{1,0:T(8,128)(2,1)}, bf16[1024,2048]{1,0:T(8,128)(2,1)}) custom-call(s32[1]{0:T(128)} %bitcast.me_ref, bf16[2048,1024]{1,0:T(8,128)(2,1)} %bitcast.4, bf16[2048,1024]{1,0:T(8,128)(2,1)} %bitcast.6), custom_call_target="tpu_custom_call" | custom-call | flops 3579139328 | bytes 20000000 | tf_op jit(solution)/shard_map/pallas_call | solution.py:89
  11.6 28.6 %shard_map.179 = (f32[2048,2560]{1,0:T(8,128)}, f32[2048,2560]{1,0:T(8,128)}, bf16[2048,2560]{1,0:T(8,128)(2,1)}) custom-call(s32[1]{0:T(128)} %bitcast.me_ref, bf16[2048,1024]{1,0:T(8,128)(2,1)} %get-tuple-element.53.a_ref, bf16[2,1024,2560]{2,1,0:T(8,128)(2,1)} %refs_8_.7, bf16[2,1024,2560]{2,1,0:T(8,128)(2,1)} %refs_9_.7), custom_call_target="tpu_custom_call" | custom-call | flops 21474836480 | bytes 67000000 | tf_op jit(solution)/shard_map/pallas_call | solution.py:104
  40.3 19.7 %shard_map.180 = (bf16[2048,1024]{1,0:T(8,128)(2,1)}, bf16[2048,1024]{1,0:T(8,128)(2,1)}, bf16[1024,2048]{1,0:T(8,128)(2,1)}) custom-call(s32[1]{0:T(128)} %bitcast.me_ref, bf16[2048,2560]{1,0:T(8,128)(2,1)} %get-tuple-element.54.act_ref, bf16[2,2560,1024]{2,1,0:T(8,128)(2,1)} %refs_10_.7, bf16[2048,1024]{1,0:T(8,128)(2,1)} %bitcast.5), custom_call_target="tpu_custom_call" | custom-call | flops 10737418240 | bytes 32000000 | tf_op jit(solution)/shard_map/pallas_call | solution.py:125
  59.9 106.5 %shard_map.181 = (bf16[3,128,2560]{2,1,0:T(8,128)(2,1)}, f32[8,128]{1,0:T(8,128)}, bf16[2048,2560]{1,0:T(8,128)(2,1)}, bf16[2048,2560]{1,0:T(8,128)(2,1)}) custom-call(bf16[2048,1024]{1,0:T(8,128)(2,1)} %bitcast.7, bf16[2048,1024]{1,0:T(8,128)(2,1)} %get-tuple-element.55.refs_1_, bf16[1024,2048]{1,0:T(8,128)(2,1)} %get-tuple-element.56.refs_2_, ...), custom_call_target="tpu_custom_call" | custom-call | flops 64424509440 | bytes 60000000 | tf_op jit(solution)/shard_map/pallas_call | solution.py:297
  166.4 2.7 fusion
  170.1 2.0 collective-permute-start.14
  173.2 33.1 %shard_map.182 = (bf16[2048,1024]{1,0:T(8,128)(2,1)}, bf16[1024,2048]{1,0:T(8,128)(2,1)}) custom-call(s32[1]{0:T(128)} %bitcast.me_ref, bf16[2048,2560]{1,0:T(8,128)(2,1)} %get-tuple-element.59.dg_ref, bf16[2048,2560]{1,0:T(8,128)(2,1)} %get-tuple-element.60.du_ref, bf16[2,1024,2560]{2,1,0:T(8,128)(2,1)} %refs_8_.7, bf16[2,1024,2560]{2,1,0:T(8,128)(2,1)} %refs_9_.7, ...), custom_call_target="tpu_custom_call" | custom-call | flops 21474836480 | bytes 48000000 | tf_op jit(solution)/shard_map/pallas_call | solution.py:323
  206.2 88.7 %shard_map.183 = (bf16[3,128,2560]{2,1,0:T(8,128)(2,1)}, f32[8,128]{1,0:T(8,128)}) custom-call(bf16[2048,1024]{1,0:T(8,128)(2,1)} %get-tuple-element.62.refs_0_, bf16[1024,2048]{1,0:T(8,128)(2,1)} %get-tuple-element.63.refs_1_, bf16[1024,2048]{1,0:T(8,128)(2,1)} %get-tuple-element.64.refs_2_, bf16[2,2560,1024]{2,1,0:T(8,128)(2,1)} %refs_10_.7, ...), custom_call_target="tpu_custom_call" | custom-call | flops 42949672960 | bytes 60000000 | tf_op jit(solution)/shard_map/pallas_call | solution.py:297
  294.9 2.6 fusion.1
  297.5 1.6 collective-permute-start.7
  301.7 20.1 %collective-permute-done.7.refs_1_ = bf16[3,128,1280]{2,1,0:T(8,128)(2,1)S(1)} collective-permute-done((bf16[3,128,1280]{2,1,0:T(8,128)(2,1)S(1)}, bf16[3,128,1280]{2,1,0:T(8,128)(2,1)S(1)}, u32[]{:S(2)}, u32[]{:S(2)}) %collective-permute-start.7) | collective-permute-done | bytes 983072 | tf_op jit(solution)/shard_map/ppermute | solution.py:391
  321.8 1.5 collective-permute-start.23
  324.3 18.7 %collective-permute-done.refs_1_ = bf16[3,128,1280]{2,1,0:T(8,128)(2,1)} collective-permute-done((bf16[3,128,1280]{2,1,0:T(8,128)(2,1)}, bf16[3,128,1280]{2,1,0:T(8,128)(2,1)}, u32[]{:S(2)}, u32[]{:S(2)}) %collective-permute-start) | collective-permute-done | bytes 983072 | tf_op jit(solution)/shard_map/ppermute | solution.py:391
  343.0 1.5 collective-permute-start.16
  344.4 8.9 %collective-permute-done.23.refs_3_ = bf16[3,128,1280]{2,1,0:T(8,128)(2,1)S(1)} collective-permute-done((bf16[3,128,1280]{2,1,0:T(8,128)(2,1)}, bf16[3,128,1280]{2,1,0:T(8,128)(2,1)S(1)}, u32[]{:S(2)}, u32[]{:S(2)}) %collective-permute-start.23) | collective-permute-done | bytes 983072 | tf_op jit(solution)/shard_map/ppermute | solution.py:391
  356.1 7.7 %collective-permute-done.16.refs_3_ = bf16[3,128,1280]{2,1,0:T(8,128)(2,1)S(1)} collective-permute-done((bf16[3,128,1280]{2,1,0:T(8,128)(2,1)}, bf16[3,128,1280]{2,1,0:T(8,128)(2,1)S(1)}, u32[]{:S(2)}, u32[]{:S(2)}) %collective-permute-start.16) | collective-permute-done | bytes 983072 | tf_op jit(solution)/shard_map/ppermute | solution.py:391
  365.8 8.6 %collective-permute-done.9.refs_3_ = bf16[3,128,1280]{2,1,0:T(8,128)(2,1)S(1)} collective-permute-done((bf16[3,128,1280]{2,1,0:T(8,128)(2,1)S(1)}, bf16[3,128,1280]{2,1,0:T(8,128)(2,1)S(1)}, u32[]{:S(2)}, u32[]{:S(2)}) %collective-permute-start.9) | collective-permute-done | bytes 983072 | tf_op jit(solution)/shard_map/ppermute | solution.py:391
  375.6 9.4 %collective-permute-done.2.refs_3_ = bf16[3,128,1280]{2,1,0:T(8,128)(2,1)} collective-permute-done((bf16[3,128,1280]{2,1,0:T(8,128)(2,1)}, bf16[3,128,1280]{2,1,0:T(8,128)(2,1)}, u32[]{:S(2)}, u32[]{:S(2)}) %collective-permute-start.2) | collective-permute-done | bytes 983072 | tf_op jit(solution)/shard_map/ppermute | solution.py:391
  386.6 1.3 add_reduce_fusion
  387.9 23.3 %psum.7 = f32[]{:T(128)} all-reduce(f32[]{:T(128)} %add_reduce_fusion), channel_id=1, replica_groups=mesh['rep'=1,'dp'=8] {'dp'}, use_global_device_ids=true, to_apply=%region_1.0 | all-reduce | flops 1 | bytes 8 | tf_op jit(solution)/shard_map/psum | solution.py:414
  411.9 31.9 %shard_map.184 = (bf16[2,1024,2560]{2,1,0:T(8,128)(2,1)}, bf16[2,1024,2560]{2,1,0:T(8,128)(2,1)}, bf16[2,2560,1024]{2,1,0:T(8,128)(2,1)}, f32[2,1024,2560]{2,1,0...) custom-call(s32[1]{0:T(128)} %bitcast.me_ref, ...), custom_call_target="tpu_custom_call" | custom-call | flops 786432000 | bytes 86507520 | tf_op jit(solution)/shard_map/pallas_call | solution.py:379
  443.8 31.9 %shard_map.185 = (bf16[2,1024,2560]{2,1,0:T(8,128)(2,1)}, bf16[2,1024,2560]{2,1,0:T(8,128)(2,1)}, bf16[2,2560,1024]{2,1,0:T(8,128)(2,1)}, f32[2,1024,2560]{2,1,0...) custom-call(s32[1]{0:T(128)} %bitcast.me_ref, ...), custom_call_target="tpu_custom_call", output_to_operand_aliasing={{0}: (19, {}), {1}: (20, {}), {2}: (21, {}), {3}: (22, {}),... | custom-call | flops 786432000 | bytes 86507520 | tf_op jit(solution)/shard_map/pallas_call | solution.py:379
  475.7 31.9 %shard_map.186 = (bf16[2,1024,2560]{2,1,0:T(8,128)(2,1)}, bf16[2,1024,2560]{2,1,0:T(8,128)(2,1)}, bf16[2,2560,1024]{2,1,0:T(8,128)(2,1)}, f32[2,1024,2560]{2,1,0...) custom-call(s32[1]{0:T(128)} %bitcast.me_ref, ...), custom_call_target="tpu_custom_call", output_to_operand_aliasing={{0}: (19, {}), {1}: (20, {}), {2}: (21, {}), {3}: (22, {}),... | custom-call | flops 786432000 | bytes 86507520 | tf_op jit(solution)/shard_map/pallas_call | solution.py:379
  507.6 31.9 %shard_map.187 = (bf16[2,1024,2560]{2,1,0:T(8,128)(2,1)}, bf16[2,1024,2560]{2,1,0:T(8,128)(2,1)}, bf16[2,2560,1024]{2,1,0:T(8,128)(2,1)}, f32[2,1024,2560]{2,1,0...) custom-call(s32[1]{0:T(128)} %bitcast.me_ref, ...), custom_call_target="tpu_custom_call", output_to_operand_aliasing={{0}: (19, {}), {1}: (20, {}), {2}: (21, {}), {3}: (22, {}),... | custom-call | flops 786432000 | bytes 86507520 | tf_op jit(solution)/shard_map/pallas_call | solution.py:379
  (80 shorter events, 13.3 us)
Async XLA Ops:
  169.1 128.4 %collective-permute-start.21 = (bf16[3,128,1280]{2,1,0:T(8,128)(2,1)}, bf16[3,128,1280]{2,1,0:T(8,128)(2,1)}, u32[]{:S(2)}, u32[]{:S(2)}) collective-permute-start(bf16[3,128,1280]{2,1,0:T(8,128)(2,1)} %get-tuple-element.97.refs_0_), channel_id=1, source_target_pairs={{0,2},{1,5},{2,0},{3,7},{4,6},{5,1},{6,4},{7,3}} | collective-permute-start | bytes 2949128 | tf_op jit(solution)/shard_map/ppermute | solution.py:391
  169.6 127.9 %collective-permute-start.22 = (bf16[3,128,1280]{2,1,0:T(8,128)(2,1)}, bf16[3,128,1280]{2,1,0:T(8,128)(2,1)}, u32[]{:S(2)}, u32[]{:S(2)}) collective-permute-start(bf16[3,128,1280]{2,1,0:T(8,128)(2,1)} %get-tuple-element.97.refs_0_), channel_id=1, source_target_pairs={{0,4},{1,3},{2,6},{3,1},{4,0},{5,7},{6,2},{7,5}} | collective-permute-start | bytes 2949128 | tf_op jit(solution)/shard_map/ppermute | solution.py:391
  170.0 129.1 %collective-permute-start.24 = (bf16[3,128,1280]{2,1,0:T(8,128)(2,1)}, bf16[3,128,1280]{2,1,0:T(8,128)(2,1)}, u32[]{:S(2)}, u32[]{:S(2)}) collective-permute-start(bf16[3,128,1280]{2,1,0:T(8,128)(2,1)} %get-tuple-element.97.refs_0_), channel_id=1, source_target_pairs={{0,1},{1,0},{2,3},{3,2},{4,5},{5,4},{6,7},{7,6}} | collective-permute-start | bytes 2949128 | tf_op jit(solution)/shard_map/ppermute | solution.py:391
  170.1 130.2 %collective-permute-start.14 = (bf16[3,128,1280]{2,1,0:T(8,128)(2,1)S(1)}, bf16[3,128,1280]{2,1,0:T(8,128)(2,1)}, u32[]{:S(2)}, u32[]{:S(2)}) collective-permute-start(bf16[3,128,1280]{2,1,0:T(8,128)(2,1)S(1)} %get-tuple-element.98.refs_0_), channel_id=1, source_target_pairs={{0,2},{1,5},{2,0},{3,7},{4,6},{5,1},{6,4},{7,3}} | collective-permute-start | bytes 2949128 | tf_op jit(solution)/shard_map/ppermute | solution.py:391
  172.1 128.2 %collective-permute-start.15 = (bf16[3,128,1280]{2,1,0:T(8,128)(2,1)S(1)}, bf16[3,128,1280]{2,1,0:T(8,128)(2,1)}, u32[]{:S(2)}, u32[]{:S(2)}) collective-permute-start(bf16[3,128,1280]{2,1,0:T(8,128)(2,1)S(1)} %get-tuple-element.98.refs_0_), channel_id=1, source_target_pairs={{0,4},{1,3},{2,6},{3,1},{4,0},{5,7},{6,2},{7,5}} | collective-permute-start | bytes 2949128 | tf_op jit(solution)/shard_map/ppermute | solution.py:391
  297.5 24.3 %collective-permute-start.7 = (bf16[3,128,1280]{2,1,0:T(8,128)(2,1)S(1)}, bf16[3,128,1280]{2,1,0:T(8,128)(2,1)S(1)}, u32[]{:S(2)}, u32[]{:S(2)}) collective-permute-start(bf16[3,128,1280]{2,1,0:T(8,128)(2,1)S(1)} %get-tuple-element.99.refs_0_), channel_id=1, source_target_pairs={{0,2},{1,5},{2,0},{3,7},{4,6},{5,1},{6,4},{7,3}} | collective-permute-start | bytes 2949128 | tf_op jit(solution)/shard_map/ppermute | solution.py:391
  299.1 24.6 %collective-permute-start.8 = (bf16[3,128,1280]{2,1,0:T(8,128)(2,1)S(1)}, bf16[3,128,1280]{2,1,0:T(8,128)(2,1)S(1)}, u32[]{:S(2)}, u32[]{:S(2)}) collective-permute-start(bf16[3,128,1280]{2,1,0:T(8,128)(2,1)S(1)} %get-tuple-element.99.refs_0_), channel_id=1, source_target_pairs={{0,4},{1,3},{2,6},{3,1},{4,0},{5,7},{6,2},{7,5}} | collective-permute-start | bytes 2949128 | tf_op jit(solution)/shard_map/ppermute | solution.py:391
  300.2 23.5 %collective-permute-start.10 = (bf16[3,128,1280]{2,1,0:T(8,128)(2,1)S(1)}, bf16[3,128,1280]{2,1,0:T(8,128)(2,1)S(1)}, u32[]{:S(2)}, u32[]{:S(2)}) collective-permute-start(bf16[3,128,1280]{2,1,0:T(8,128)(2,1)S(1)} %get-tuple-element.99.refs_0_), channel_id=1, source_target_pairs={{0,1},{1,0},{2,3},{3,2},{4,5},{5,4},{6,7},{7,6}} | collective-permute-start | bytes 2949128 | tf_op jit(solution)/shard_map/ppermute | solution.py:391
  300.2 42.7 %collective-permute-start = (bf16[3,128,1280]{2,1,0:T(8,128)(2,1)}, bf16[3,128,1280]{2,1,0:T(8,128)(2,1)}, u32[]{:S(2)}, u32[]{:S(2)}) collective-permute-start(bf16[3,128,1280]{2,1,0:T(8,128)(2,1)} %get-tuple-element.100.refs_0_), channel_id=1, source_target_pairs={{0,2},{1,5},{2,0},{3,7},{4,6},{5,1},{6,4},{7,3}} | collective-permute-start | bytes 2949128 | tf_op jit(solution)/shard_map/ppermute | solution.py:391
  300.8 43.6 %collective-permute-start.1 = (bf16[3,128,1280]{2,1,0:T(8,128)(2,1)}, bf16[3,128,1280]{2,1,0:T(8,128)(2,1)}, u32[]{:S(2)}, u32[]{:S(2)}) collective-permute-start(bf16[3,128,1280]{2,1,0:T(8,128)(2,1)} %get-tuple-element.100.refs_0_), channel_id=1, source_target_pairs={{0,4},{1,3},{2,6},{3,1},{4,0},{5,7},{6,2},{7,5}} | collective-permute-start | bytes 2949128 | tf_op jit(solution)/shard_map/ppermute | solution.py:391
  321.8 31.5 %collective-permute-start.23 = (bf16[3,128,1280]{2,1,0:T(8,128)(2,1)}, bf16[3,128,1280]{2,1,0:T(8,128)(2,1)S(1)}, u32[]{:S(2)}, u32[]{:S(2)}) collective-permute-start(bf16[3,128,1280]{2,1,0:T(8,128)(2,1)} %collective-permute-done.21.refs_1_), channel_id=1, source_target_pairs={{0,4},{1,3},{2,6},{3,1},{4,0},{5,7},{6,2},{7,5}} | collective-permute-start | bytes 2949128 | tf_op jit(solution)/shard_map/ppermute | solution.py:391
  323.8 30.2 %collective-permute-start.25 = (bf16[3,128,1280]{2,1,0:T(8,128)(2,1)}, bf16[3,128,1280]{2,1,0:T(8,128)(2,1)S(1)}, u32[]{:S(2)}, u32[]{:S(2)}) collective-permute-start(bf16[3,128,1280]{2,1,0:T(8,128)(2,1)} %collective-permute-done.21.refs_1_), channel_id=1, source_target_pairs={{0,1},{1,0},{2,3},{3,2},{4,5},{5,4},{6,7},{7,6}} | collective-permute-start | bytes 2949128 | tf_op jit(solution)/shard_map/ppermute | solution.py:391
  323.8 31.3 %collective-permute-start.26 = (bf16[3,128,1280]{2,1,0:T(8,128)(2,1)}, bf16[3,128,1280]{2,1,0:T(8,128)(2,1)S(1)}, u32[]{:S(2)}, u32[]{:S(2)}) collective-permute-start(bf16[3,128,1280]{2,1,0:T(8,128)(2,1)} %collective-permute-done.22.refs_2_), channel_id=1, source_target_pairs={{0,1},{1,0},{2,3},{3,2},{4,5},{5,4},{6,7},{7,6}} | collective-permute-start | bytes 2949128 | tf_op jit(solution)/shard_map/ppermute | solution.py:391
  343.0 20.8 %collective-permute-start.16 = (bf16[3,128,1280]{2,1,0:T(8,128)(2,1)}, bf16[3,128,1280]{2,1,0:T(8,128)(2,1)S(1)}, u32[]{:S(2)}, u32[]{:S(2)}) collective-permute-start(bf16[3,128,1280]{2,1,0:T(8,128)(2,1)} %collective-permute-done.14.refs_1_), channel_id=1, source_target_pairs={{0,4},{1,3},{2,6},{3,1},{4,0},{5,7},{6,2},{7,5}} | collective-permute-start | bytes 2949128 | tf_op jit(solution)/shard_map/ppermute | solution.py:391
  344.4 20.0 %collective-permute-start.18 = (bf16[3,128,1280]{2,1,0:T(8,128)(2,1)}, bf16[3,128,1280]{2,1,0:T(8,128)(2,1)S(1)}, u32[]{:S(2)}, u32[]{:S(2)}) collective-permute-start(bf16[3,128,1280]{2,1,0:T(8,128)(2,1)} %collective-permute-done.14.refs_1_), channel_id=1, source_target_pairs={{0,1},{1,0},{2,3},{3,2},{4,5},{5,4},{6,7},{7,6}} | collective-permute-start | bytes 2949128 | tf_op jit(solution)/shard_map/ppermute | solution.py:391
  353.9 20.4 %collective-permute-start.9 = (bf16[3,128,1280]{2,1,0:T(8,128)(2,1)S(1)}, bf16[3,128,1280]{2,1,0:T(8,128)(2,1)S(1)}, u32[]{:S(2)}, u32[]{:S(2)}) collective-permute-start(bf16[3,128,1280]{2,1,0:T(8,128)(2,1)S(1)} %collective-permute-done.7.refs_1_), channel_id=1, source_target_pairs={{0,4},{1,3},{2,6},{3,1},{4,0},{5,7},{6,2},{7,5}} | collective-permute-start | bytes 2949128 | tf_op jit(solution)/shard_map/ppermute | solution.py:391
  355.1 20.0 %collective-permute-start.11 = (bf16[3,128,1280]{2,1,0:T(8,128)(2,1)S(1)}, bf16[3,128,1280]{2,1,0:T(8,128)(2,1)S(1)}, u32[]{:S(2)}, u32[]{:S(2)}) collective-permute-start(bf16[3,128,1280]{2,1,0:T(8,128)(2,1)S(1)} %collective-permute-done.7.refs_1_), channel_id=1, source_target_pairs={{0,1},{1,0},{2,3},{3,2},{4,5},{5,4},{6,7},{7,6}} | collective-permute-start | bytes 2949128 | tf_op jit(solution)/shard_map/ppermute | solution.py:391
  364.4 20.5 %collective-permute-start.2 = (bf16[3,128,1280]{2,1,0:T(8,128)(2,1)}, bf16[3,128,1280]{2,1,0:T(8,128)(2,1)}, u32[]{:S(2)}, u32[]{:S(2)}) collective-permute-start(bf16[3,128,1280]{2,1,0:T(8,128)(2,1)} %collective-permute-done.refs_1_), channel_id=1, source_target_pairs={{0,4},{1,3},{2,6},{3,1},{4,0},{5,7},{6,2},{7,5}} | collective-permute-start | bytes 2949128 | tf_op jit(solution)/shard_map/ppermute | solution.py:391
  365.6 19.7 %collective-permute-start.27 = (bf16[3,128,1280]{2,1,0:T(8,128)(2,1)S(1)}, bf16[3,128,1280]{2,1,0:T(8,128)(2,1)S(1)}, u32[]{:S(2)}, u32[]{:S(2)}) collective-permute-start(bf16[3,128,1280]{2,1,0:T(8,128)(2,1)S(1)} %collective-permute-done.23.refs_3_), channel_id=1, source_target_pairs={{0,1},{1,0},{2,3},{3,2},{4,5},{5,4},{6,7},{7,6}} | collective-permute-start | bytes 2949128 | tf_op jit(solution)/shard_map/ppermute | solution.py:391
  375.1 100.6 %collective-permute-start.13 = (bf16[3,128,1280]{2,1,0:T(8,128)(2,1)S(1)}, bf16[3,128,1280]{2,1,0:T(8,128)(2,1)}, u32[]{:S(2)}, u32[]{:S(2)}) collective-permute-start(bf16[3,128,1280]{2,1,0:T(8,128)(2,1)S(1)} %collective-permute-done.9.refs_3_), channel_id=1, source_target_pairs={{0,1},{1,0},{2,3},{3,2},{4,5},{5,4},{6,7},{7,6}} | collective-permute-start | bytes 2949128 | tf_op jit(solution)/shard_map/ppermute | solution.py:391
  375.2 132.5 %collective-permute-start.3 = (bf16[3,128,1280]{2,1,0:T(8,128)(2,1)}, bf16[3,128,1280]{2,1,0:T(8,128)(2,1)}, u32[]{:S(2)}, u32[]{:S(2)}) collective-permute-start(bf16[3,128,1280]{2,1,0:T(8,128)(2,1)} %get-tuple-element.100.refs_0_), channel_id=1, source_target_pairs={{0,1},{1,0},{2,3},{3,2},{4,5},{5,4},{6,7},{7,6}} | collective-permute-start | bytes 2949128 | tf_op jit(solution)/shard_map/ppermute | solution.py:391
  385.0 122.6 %collective-permute-start.4 = (bf16[3,128,1280]{2,1,0:T(8,128)(2,1)}, bf16[3,128,1280]{2,1,0:T(8,128)(2,1)}, u32[]{:S(2)}, u32[]{:S(2)}) collective-permute-start(bf16[3,128,1280]{2,1,0:T(8,128)(2,1)} %collective-permute-done.refs_1_), channel_id=1, source_target_pairs={{0,1},{1,0},{2,3},{3,2},{4,5},{5,4},{6,7},{7,6}} | collective-permute-start | bytes 2949128 | tf_op jit(solution)/shard_map/ppermute | solution.py:391
  385.3 122.3 %collective-permute-start.5 = (bf16[3,128,1280]{2,1,0:T(8,128)(2,1)}, bf16[3,128,1280]{2,1,0:T(8,128)(2,1)}, u32[]{:S(2)}, u32[]{:S(2)}) collective-permute-start(bf16[3,128,1280]{2,1,0:T(8,128)(2,1)} %collective-permute-done.1.refs_2_), channel_id=1, source_target_pairs={{0,1},{1,0},{2,3},{3,2},{4,5},{5,4},{6,7},{7,6}} | collective-permute-start | bytes 2949128 | tf_op jit(solution)/shard_map/ppermute | solution.py:391
  385.5 122.1 %collective-permute-start.6 = (bf16[3,128,1280]{2,1,0:T(8,128)(2,1)}, bf16[3,128,1280]{2,1,0:T(8,128)(2,1)}, u32[]{:S(2)}, u32[]{:S(2)}) collective-permute-start(bf16[3,128,1280]{2,1,0:T(8,128)(2,1)} %collective-permute-done.2.refs_3_), channel_id=1, source_target_pairs={{0,1},{1,0},{2,3},{3,2},{4,5},{5,4},{6,7},{7,6}} | collective-permute-start | bytes 2949128 | tf_op jit(solution)/shard_map/ppermute | solution.py:391
  (21 other events, 571.5 us)

commit v2 on v1

v2 whole, which is shorter than its diff:
```python
import jax
import jax.numpy as jnp
from jax import lax
from jax.experimental import pallas as pl
from jax.experimental.pallas import tpu as pltpu
from jax.sharding import PartitionSpec as P


T, D, F, L = 2048, 1024, 2560, 2
FT = 256
BLK = 128
SUB = 512
HALVES = (0, F // 2)
WIDE = F // 2
F32, BF16 = jnp.float32, jnp.bfloat16
MB = 1 << 20

NT = (((1,), (1,)), ((), ()))


def dot(a, b):
    return jnp.dot(a, b, preferred_element_type=F32)


def dot_nt(a, b):
    return lax.dot_general(a, b, NT, preferred_element_type=F32)


def sigmoid(x):
    return 0.5 * jnp.tanh(0.5 * x) + 0.5


def normed(h):
    wide = h.astype(F32)
    scale = lax.rsqrt(jnp.mean(wide * wide, -1, keepdims=True) + 1e-6)
    return (wide * scale).astype(BF16)


def place(shard, me):
    sx, sy, half = (flip + (1 - 2 * flip) * bit for bit, flip in zip((me // 4, (me // 2) % 2, me % 2), (shard >> 2, (shard >> 1) & 1, shard & 1)))
    return half * 4 + (sy * 2 + sx if shard & 1 else sx * 2 + sy)


def shard_at(p, me):
    half, k = p >> 2, p & 3
    hi, lo = k >> 1, k & 1
    core = (me & 1) ^ half
    sx, sy = (1 - core) * hi + core * lo, (1 - core) * lo + core * hi
    return me ^ (sx * 4 + sy * 2 + half)


def store_turned(me, tile, out_ref, columns=slice(None)):
    for shard in range(8):
        rows = pl.ds(pl.multiple_of(place(shard, me) * BLK, BLK), BLK)
        out_ref[rows, columns] = tile[:, shard * BLK : (shard + 1) * BLK].T


def call(kernel, grid, ins, outs, scratch=(), flops=0, moved=0, aliases=None):
    return pl.pallas_call(
        kernel,
        grid_spec=pltpu.PrefetchScalarGridSpec(num_scalar_prefetch=1, grid=grid, in_specs=[s for s in ins], out_specs=[s for s, _ in outs], scratch_shapes=list(scratch)),
        out_shape=[o for _, o in outs],
        compiler_params=pltpu.CompilerParams(dimension_semantics=("arbitrary",) * len(grid), vmem_limit_bytes=63 * MB),
        cost_estimate=pl.CostEstimate(flops=int(flops), bytes_accessed=int(moved), transcendentals=0),
        input_output_aliases=aliases or {},
    )


def shaped(shape, dtype=BF16):
    return jax.ShapeDtypeStruct(shape, dtype)


MM = 2 * T * D * F


def gate_up(me, x, w_gate, w_up):
    def kernel(me_ref, x_ref, wg_ref, wu_ref, g_ref, u_ref, act_ref, a_ref):
        @pl.when(pl.program_id(0) == 0)
        def _():
            for t in range(T // SUB):
                rows = slice(t * SUB, (t + 1) * SUB)
                a_ref[rows, :] = normed(x_ref[rows, :])

        for t in range(T // SUB):
            rows = slice(t * SUB, (t + 1) * SUB)
            g = dot(a_ref[rows], wg_ref[0])
            u = dot(a_ref[rows], wu_ref[0])
            g_ref[rows, :] = g
            u_ref[rows, :] = u
            act_ref[rows, :] = (g * sigmoid(g) * u).astype(BF16)

    weight = pl.BlockSpec((1, D, FT), lambda j, m: (0, 0, j))
    tile = pl.BlockSpec((T, FT), lambda j, m: (0, j))
    return call(
        kernel,
        (F // FT,),
        [pl.BlockSpec((T, D), lambda j, m: (0, 0), pipeline_mode=pl.Buffered(1)), weight, weight],
        [(tile, shaped((T, F), F32)), (tile, shaped((T, F), F32)), (tile, shaped((T, F)))],
        [pltpu.VMEM((T, D), BF16)],
        flops=2 * MM,
        moved=67e6,
    )(me, x, w_gate, w_up)


def down(me, act, w_down, x, dy):
    rows = 512

    def kernel(me_ref, act_ref, wd_ref, x_ref, dy_ref, out_ref, a_ref, at_ref, a0t_ref, dyt_ref):
        store_turned(me_ref[0], normed(x_ref[...]), a0t_ref)
        store_turned(me_ref[0], dy_ref[...], dyt_ref)
        out = x_ref[...] + dot(act_ref[...], wd_ref[0]).astype(BF16)
        out_ref[...] = out
        a = normed(out)
        a_ref[...] = a
        store_turned(me_ref[0], a, at_ref)

    tall = pl.BlockSpec((rows, D), lambda i, m: (i, 0))
    flat = pl.BlockSpec((D, rows), lambda i, m: (0, i))
    return call(
        kernel,
        (T // rows,),
        [pl.BlockSpec((rows, F), lambda i, m: (i, 0)), pl.BlockSpec((1, F, D), lambda i, m: (0, 0, 0), pipeline_mode=pl.Buffered(1)), tall, tall],
        [(tall, shaped((T, D))), (tall, shaped((T, D)))] + [(flat, shaped((D, T)))] * 3,
        flops=MM,
        moved=44e6,
    )(me, act, w_down, x, dy)


def both(a, b):
    return (a.astype(F32) + b.astype(F32)).astype(BF16)


def backward(dy, a1, a1t, dyt, h, a0t, gate, up, w_gate, w_up, w_down):
    n = F // FT
    mid = n // 2
    turn, low = n, n + 1
    end = low + n
    steps = end + 7

    def kernel(*refs):
        refs = list(refs)
        take = lambda count: [refs.pop(0) for _ in range(count)]
        dy_ref, a1_ref, a1t_ref, dyt_ref, h_ref, a0t_ref = take(6)
        wd_ref, wg_ref, wu_ref, g_ref, u_ref = take(5)
        owns = take(4)
        got_ref, factor_ref = take(2)
        dg_ref, du_ref, act_ref = take(3)
        dh_v, a_v, at_v, dht_v, acc = take(5)
        keep, send, recv0, away1, stay1, recv1, away2, stay2, recv2, own_v = take(10)
        sq_ref, all_sq = take(2)
        sems, s0, r0, s1, r1, s2, r2, s3, r3, s4, r4, s5, r5, s6, r6 = take(15)
        pairs = ((dy_ref, dh_v), (a1_ref, a_v), (a1t_ref, at_v), (dyt_ref, dht_v), (h_ref, a_v), (a0t_ref, at_v))
        copies = [pltpu.make_async_copy(s, d, sems.at[i]) for i, (s, d) in enumerate(pairs)]
        j = pl.program_id(0)
        me = lax.axis_index("dp")
        core = me % 2
        other = me + 1 - 2 * core
        xs, ys = me + 4 - 8 * (me // 4), me + 2 - 4 * ((me // 2) % 2)
        near, far = (1 - core) * xs + core * ys, (1 - core) * ys + core * xs

        def remote(src, dst, ss, rs, to):
            return pltpu.make_async_remote_copy(src, dst, ss, rs, device_id={"dp": to}, device_id_type=pl.DeviceIdType.MESH)

        def core_copy(t):
            return remote(send.at[t % 2], recv0.at[t % 3], s0.at[t % 2], r0.at[t % 3], other)

        def near_copy(t):
            return remote(away1.at[t % 2], recv1.at[t % 5], s1.at[t % 2], r1.at[t % 5], near)

        def far_copy(t):
            return remote(away2.at[t % 2], recv2.at[t % 5], s2.at[t % 2], r2.at[t % 5], far)

        def place_of(k, t):
            return got_ref.at[k - 1, :, :, pl.ds(pl.multiple_of(t * FT, FT), FT)]

        def gather_far(t):
            return remote(own_v.at[t], place_of(1, t), s3.at[t], r3.at[t], far)

        def gather_near(t):
            return (remote(own_v.at[t], place_of(2, t), s4.at[t], r4.at[t], near), remote(place_of(1, t), place_of(3, t), s5.at[t], r5.at[t], near))

        def tell(o):
            return remote(sq_ref, all_sq.at[me], s6.at[o - 1], r6.at[me], (me + o) % 8)

        def told(o):
            return remote(sq_ref, all_sq.at[(me + o) % 8], s6.at[o - 1], r6.at[(me + o) % 8], (me + o) % 8)

        def between(first, count):
            return (j >= first) & (j < first + count)

        def behind(steps):
            return between(steps, n) | between(low + steps, n)

        barrier = pltpu.get_barrier_semaphore()

        @pl.when(j == 0)
        def _():
            for o in range(1, 8):
                pl.semaphore_signal(barrier, inc=1, device_id={"dp": (me + o) % 8}, device_id_type=pl.DeviceIdType.MESH)
            for c in copies[:4]:
                c.start()
            sq_ref[...] = jnp.zeros_like(sq_ref)

        @pl.when(between(10, mid))
        def _():
            for c in gather_near(j - 10):
                c.wait()

        @pl.when(between(8, mid))
        def _():
            gather_far(j - 8).wait()

        def finish(out, number):
            t = j - 6
            far_copy(t).wait()
            for i in range(3):
                done = both(stay2[t % 2, i], recv2[t % 5, i])
                out[i] = done
                if number == 0:
                    own_v[t, i] = done
                done = done.astype(F32)
                done = jnp.sum((done * done).reshape(BLK // 8, 8, FT), 0)
                sq_ref[...] += done[:, :128] + done[:, 128:]

        for number, first in enumerate((0, mid, low, low + mid)):

            @pl.when(between(first + 6, mid))
            def _(number=number):
                finish(owns[number], number)

        @pl.when(behind(4))
        def _():
            t = j - 4
            near_copy(t).wait()
            for i in range(3):
                away2[t % 2, i] = both(stay1[t % 2, 1, i], recv1[t % 5, 1, i])
                stay2[t % 2, i] = both(stay1[t % 2, 0, i], recv1[t % 5, 0, i])

        @pl.when(behind(2))
        def _():
            t = j - 2
            core_copy(t).wait()
            for k in range(2):
                for i in range(3):
                    away1[t % 2, k, i] = both(keep[t % 2, 2 + k, i], recv0[t % 3, 2 + k, i])
                    stay1[t % 2, k, i] = both(keep[t % 2, k, i], recv0[t % 3, k, i])

        def tokens(t, upper):
            rows = slice(t * SUB, (t + 1) * SUB)
            if upper:
                g, u = dot(a_v[rows], wg_ref[0]), dot(a_v[rows], wu_ref[0])
            else:
                g, u = g_ref[rows, :], u_ref[rows, :]
            dact = dot_nt(dh_v[rows], wd_ref[0]).astype(BF16).astype(F32)
            s = sigmoid(g)
            gs = g * s
            act_ref[rows, :] = (gs * u).astype(BF16)
            du_ref[rows, :] = (dact * gs).astype(BF16)
            dg_ref[rows, :] = (dact * u * (s + gs * (1.0 - s))).astype(BF16)

        def by_input(t):
            rows = slice(t * SUB, (t + 1) * SUB)
            da = acc[rows, :].astype(BF16).astype(F32)
            wide = a_v[rows, :].astype(F32)
            scale = lax.rsqrt(jnp.mean(wide * wide, -1, keepdims=True) + 1e-6)
            along = jnp.mean(da * wide, -1, keepdims=True) * (scale * scale * scale)
            out = dh_v[rows, :] + (da * scale - wide * along).astype(BF16)
            dh_v[rows, :] = out
            store_turned(me, out, dht_v, rows)

        @pl.when(j == 0)
        def _():
            for c in copies[:2]:
                c.wait()

        @pl.when(j == turn)
        def _():
            copies[5].start()
            copies[4].wait()

        def work(some):
            @pl.when(j < n)
            def _():
                for t in some:
                    tokens(t, True)

            @pl.when(j == turn)
            def _():
                for t in some:
                    by_input(t)

            @pl.when(between(low, n))
            def _():
                for t in some:
                    tokens(t, False)

        work((0,))

        @pl.when(j == 0)
        def _():
            pl.semaphore_wait(barrier, 7)

        @pl.when(j == steps - 1)
        def _():
            for o in range(1, 8):
                tell(o).start()
            all_sq[me] = sq_ref[...]
            for o in range(1, 8):
                tell(o).wait_send()
                told(o).wait_recv()
            total = all_sq[0]
            for d in range(1, 8):
                total = total + all_sq[d]
            total = jnp.sum(jnp.sum(total, 0, keepdims=True), 1, keepdims=True)
            factor = jnp.minimum(1.0, 0.5 * lax.rsqrt(total / (3 * L * D * F) + 1e-30))
            factor_ref[...] = jnp.broadcast_to(factor, (8, 128))

        @pl.when(behind(4))
        def _():
            far_copy(j - 4).start()

        @pl.when(behind(2))
        def _():
            near_copy(j - 2).start()

        @pl.when(behind(1))
        def _():
            core_copy(j - 1).start()

        @pl.when(between(6, mid))
        def _():
            gather_far(j - 6).start()

        @pl.when(between(8, mid))
        def _():
            for c in gather_near(j - 8):
                c.start()

        work(range(1, T // SUB))

        @pl.when(j == n - 1)
        def _():
            copies[4].start()

        @pl.when(j == 0)
        def _():
            for c in copies[2:4]:
                c.wait()

        @pl.when(j == low)
        def _():
            copies[5].wait()

        @pl.when(behind(0))
        def _():
            for i, (left, right) in enumerate(((at_v, dg_ref), (at_v, du_ref), (dht_v, act_ref))):
                for half, out in enumerate((keep, send)):
                    made = dot(left[half * 4 * BLK : (half + 1) * 4 * BLK, :], right[...]).astype(BF16)
                    for k in range(4):
                        out[j % 2, k, i] = made[k * BLK : (k + 1) * BLK]

        def gather_input(first):
            for t in range(T // SUB):
                rows = slice(t * SUB, (t + 1) * SUB)
                more = dot_nt(dg_ref[rows], wg_ref[0]) + dot_nt(du_ref[rows], wu_ref[0])
                acc[rows, :] = more if first else acc[rows, :] + more

        @pl.when(j == 0)
        def _():
            gather_input(True)

        @pl.when(between(1, n - 1))
        def _():
            gather_input(False)

    last = n - 1
    lower = lambda j: jnp.clip(j - low, 0, last)
    whole = pl.BlockSpec(memory_space=pl.ANY)
    weight = pl.BlockSpec((1, D, FT), lambda j: (1, 0, jnp.minimum(j, last)))
    wdown = pl.BlockSpec((1, FT, D), lambda j: (jnp.where(j < n, 1, 0), jnp.where(j < n, j, lower(j)), 0))
    tile = pl.BlockSpec((T, FT), lambda j: (0, lower(j)))

    def shard(first):
        return pl.BlockSpec((3, BLK, FT), lambda j: (0, 0, jnp.clip(j - 6 - first, 0, mid - 1))), shaped((3, BLK, WIDE))

    outs = [shard(first) for first in (0, mid, low, low + mid)]
    outs += [(whole, shaped((3, 3, BLK, WIDE))), (pl.BlockSpec((8, 128), lambda j: (0, 0)), shaped((8, 128), F32))]
    sem = pltpu.SemaphoreType.DMA
    quarter = lambda *lead: pltpu.VMEM((*lead, 3, BLK, FT), BF16)
    scratch = [pltpu.VMEM((T, FT), BF16)] * 3
    scratch += [pltpu.VMEM((T, D), BF16)] * 2 + [pltpu.VMEM((D, T), BF16)] * 2 + [pltpu.VMEM((T, D), F32)]
    scratch += [quarter(2, 4), quarter(2, 4), quarter(3, 4), quarter(2, 2), quarter(2, 2), quarter(5, 2), quarter(2), quarter(2), quarter(5), quarter(mid)]
    scratch += [pltpu.VMEM((8, 128), F32), pltpu.VMEM((8, 8, 128), F32)]
    scratch += [sem((k,)) for k in (6, 2, 3, 2, 5, 2, 5, mid, mid, mid, mid, mid, mid, 7, 8)]
    return pl.pallas_call(
        kernel,
        grid_spec=pltpu.PrefetchScalarGridSpec(
            num_scalar_prefetch=0, grid=(steps,), in_specs=[whole] * 6 + [wdown, weight, weight, tile, tile], out_specs=[s for s, _ in outs], scratch_shapes=scratch
        ),
        out_shape=[o for _, o in outs],
        compiler_params=pltpu.CompilerParams(dimension_semantics=("arbitrary",), vmem_limit_bytes=63 * MB, collective_id=0, has_side_effects=True),
        cost_estimate=pl.CostEstimate(flops=12 * MM, bytes_accessed=120_000_000, transcendentals=0),
        name="backward",
    )(dy, a1, a1t, dyt, h, a0t, w_down, w_gate, w_up, gate, up)


def adamw(me, layer, first, width, base, factor, parts, w, m, v, so_far):
    ft = 640
    steps, at0, part0 = width // ft, first // ft, (first - base) // ft

    def kernel(me_ref, f_ref, *refs):
        parts, refs = refs[:8], refs[8:]
        ws, ms, vs = refs[0:3], refs[3:6], refs[6:9]
        nws, nms, nvs, part = refs[-10:-7], refs[-7:-4], refs[-4:-1], refs[-1]
        f = f_ref[0:1, 0:1]
        p = pl.program_id(0)
        for at in range(8):

            @pl.when(p == at)
            def _(at=at):
                part[...] = parts[at][...]

        def take(i, rows, g):
            g = g.astype(F32) * f
            new_m = 0.9 * ms[i][0, rows, :] + 0.1 * g
            new_v = 0.95 * vs[i][0, rows, :] + 0.05 * g * g
            wide = ws[i][0, rows, :].astype(F32)
            nws[i][0, rows, :] = (wide - 0.02 * (new_m * lax.rsqrt(new_v + 1e-8) + 0.1 * wide)).astype(BF16)
            nms[i][0, rows, :] = new_m
            nvs[i][0, rows, :] = new_v

        for r in range(0, BLK, 16):
            for i in range(2):
                take(i, slice(r, r + 16), part[i, r : r + 16, :])
        for r in range(0, ft, 128):
            take(2, slice(r, r + 128), part[2, :, r : r + 128].T)

    def piece(at):
        where = lambda p, j: part0 + jnp.where(p == at, j, jnp.where(p < at, 0, steps - 1))
        if parts[at][1] is None:
            return pl.BlockSpec((3, BLK, ft), lambda p, j, me_ref: (0, 0, where(p, j)))
        return pl.BlockSpec((None, 3, BLK, ft), lambda p, j, me_ref: (parts[at][1], 0, 0, where(p, j)))

    across = pl.BlockSpec((1, BLK, ft), lambda p, j, me_ref: (layer, shard_at(p, me_ref[0]), at0 + j))
    along = pl.BlockSpec((1, ft, BLK), lambda p, j, me_ref: (layer, at0 + j, shard_at(p, me_ref[0])))
    three = [across, across, along]
    whole = pl.BlockSpec(memory_space=pl.ANY)
    ins = [pl.BlockSpec((8, 128), lambda p, j, me_ref: (0, 0))] + [piece(at) for at in range(8)] + three * 3
    args = [factor] + [a for a, _ in parts] + list(w) + list(m) + list(v)
    outs = [(s, shaped(o.shape, o.dtype)) for s, o in zip(three * 3, list(w) + list(m) + list(v))]
    aliases = {}
    if so_far is not None:
        aliases = {1 + len(ins) + i: i for i in range(9)}
        ins, args = ins + [whole] * 9, args + list(so_far)
    size = 3 * width * D
    return call(kernel, (8, steps), ins, outs, [pltpu.VMEM((3, BLK, ft), BF16)], flops=size * 200, moved=size * 22, aliases=aliases)(me, *args)


CORE = [(i, i ^ 1) for i in range(8)]
FIRST = [(i, i ^ (2 if i & 1 else 4)) for i in range(8)]
SECOND = [(i, i ^ (4 if i & 1 else 2)) for i in range(8)]


STAGES = {"core": CORE, "first": FIRST, "second": SECOND}


def swap(a, stage):
    return lax.ppermute(a, "dp", STAGES[stage])


def gather(own):
    mine = [own, swap(own, "second")]
    mine += [swap(a, "first") for a in mine]
    return [(a, None) for a in mine + [swap(a, "core") for a in mine]]


def solution(mesh):
    def work(x, dy, *arrays):
        weights, m, v = (arrays[i : i + 3] for i in (0, 3, 6))
        w_gate, w_up, w_down = weights
        x, dy = x[0], dy[0]
        me = lax.axis_index("dp").astype(jnp.int32).reshape(1)
        gate, up, act = gate_up(me, x, w_gate, w_up)
        h, a1, a1t, a0t, dyt = down(me, act, w_down, x, dy)
        own1a, own1b, own0a, own0b, got, factor = backward(dy, a1, a1t, dyt, h, a0t, gate, up, *weights)

        parts = [(own1a, None)] + [(got, k) for k in range(3)]
        across = swap(own1a, "core"), swap(got, "core")
        parts += [(across[0], None)] + [(across[1], k) for k in range(3)]
        new = None
        for first in (0, WIDE // 2):
            new = adamw(me, 1, first, WIDE // 2, 0, factor, parts, weights, m, v, new)
        for layer, number, own in ((1, 1, own1b), (0, 0, own0a), (0, 1, own0b)):
            parts = gather(own)
            new = adamw(me, layer, HALVES[number], WIDE, HALVES[number], factor, parts, weights, m, v, new)
        return tuple(new)

    return jax.shard_map(
        work,
        mesh=mesh,
        in_specs=(P(("rep", "dp"), None, None),) * 2 + (P(None, None, None),) * 9,
        out_specs=(P("rep", None, None),) * 9,
        check_vma=False,
    )
```

time: 541 us -> 506 us (0.935)
  blocking collectives: 23.3 us -> 0 us
  waiting for transfers between devices: 73.9 us -> 88.2 us
  Pallas kernels: 415 us -> 404 us
  starting transfers between devices: 17.6 us -> 10.7 us
  local copies, waits for them, and re-layouts: 6.9 us -> 0.82 us
    psum x1 -> x0, blocking collectives: 23.3 us -> none  [work(): squares = lax.psum(jnp.sum(squares1 + squares0), 'dp')]
    pallas_call x5 -> x2, Pallas kernels: 268 us -> 252 us  [the longest x1 222 us: backward(): pl.pallas_call(kernel, grid_spec=pltpu.PrefetchScalarGridSpec(num_scalar_...]
    ppermute x28 -> x23, waiting for transfers between devices: 73.9 us -> 88.2 us  [swap(): return lax.ppermute(a, 'dp', STAGES[stage])]
    ppermute x28 -> x23, starting transfers between devices: 17.6 us -> 10.7 us  [swap(): return lax.ppermute(a, 'dp', STAGES[stage])]
    pallas_call x4 -> x5, Pallas kernels: 128 us -> 129 us  [adamw(): call(kernel, (8, steps), ins, outs, [pltpu.VMEM((3, BLK, ft), BF16)], flo...]
  transfers between devices with their start and end apart: 28 -> 23, of which waited for: 7 -> 8; matrix products, arithmetic and copies ran while one was open for 1% -> 0% of each run, Pallas kernels for 40% -> 19%
where the time goes in v2:
time: 506 us; the launch traced here: 505 us
  Pallas kernels  404 us (80%)
  waiting for transfers between devices  88.2 us (17%)
  starting transfers between devices  10.7 us (2%)
    pallas_call x1, Pallas kernels, backward(): pl.pallas_call(kernel, grid_spec=pltpu.PrefetchScalarGridSpec(num_scalar_...  222 us
    pallas_call x5, Pallas kernels, adamw(): call(kernel, (8, steps), ins, outs, [pltpu.VMEM((3, BLK, ft), BF16)], flo...  129 us
    ppermute x23, waiting for transfers between devices, swap(): return lax.ppermute(a, 'dp', STAGES[stage])  88.2 us
    pallas_call x1, Pallas kernels, gate_up(): call(kernel, (F // FT,), [pl.BlockSpec((T, D), lambda j, m: (0, 0), pipel...  30.1 us
    pallas_call x1, Pallas kernels, down(): call(kernel, (T // rows,), [pl.BlockSpec((rows, F), lambda i, m: (i, 0)),...  22.6 us
    ppermute x23, starting transfers between devices, swap(): return lax.ppermute(a, 'dp', STAGES[stage])  10.7 us
  transfers between devices with their start and end apart: 23, of which 8 were waited for; matrix products, arithmetic and copies ran while one was open for 0% of the time, Pallas kernels for 19%

profile of v2, /device:TPU:0, one launch (start us, length us, event | category | flops | bytes accessed | tf_op | source)
XLA Modules:
  0.0 504.6 jit_solution(16285956870899908155)
XLA Ops:
  0.6 30.1 %shard_map.178 = (f32[2048,2560]{1,0:T(8,128)}, f32[2048,2560]{1,0:T(8,128)}, bf16[2048,2560]{1,0:T(8,128)(2,1)}) custom-call(s32[1]{0:T(128)} %bitcast.me_ref, bf16[2048,1024]{1,0:T(8,128)(2,1)} %bitcast.3, bf16[2,1024,2560]{2,1,0:T(8,128)(2,1)} %refs_8_.11, bf16[2,1024,2560]{2,1,0:T(8,128)(2,1)} %refs_9_.9), custom_call_target="tpu_custom_call" | custom-call | flops 21474836480 | bytes 67000000 | tf_op jit(solution)/shard_map/pallas_call | solution.py:94
  30.8 22.6 %shard_map.179 = (bf16[2048,1024]{1,0:T(8,128)(2,1)}, bf16[2048,1024]{1,0:T(8,128)(2,1)}, bf16[1024,2048]{1,0:T(8,128)(2,1)}, bf16[1024,2048]{1,0:T(8,128)(2,1)}, bf16[1024,2048]{1,0:T(8,128)(2,1)}) custom-call(s32[1]{0:T(128)} %bitcast.me_ref, bf16[2048,2560]{1,0:T(8,128)(2,1)} %get-tuple-element.59.act_ref, bf16[2,2560,1024]{2,1,0:T(8,128)(2,1)} %refs_10_.9, ...), custom_call_target="tpu_custom_call" | custom-call | flops 10737418240 | bytes 44000000 | tf_op jit(solution)/shard_map/pallas_call | solution.py:119
  53.4 221.7 %backward.1 = (bf16[3,128,1280]{2,1,0:T(8,128)(2,1)}, bf16[3,128,1280]{2,1,0:T(8,128)(2,1)}, bf16[3,128,1280]{2,1,0:T(8,128)(2,1)}, bf16[3,128,1280]{2,1,0:T(8,1...) custom-call(bf16[2048,1024]{1,0:T(8,128)(2,1)} %bitcast.6, bf16[2048,1024]{1,0:T(8,128)(2,1)} %get-tuple-element.60.refs_1_, ...), custom_call_target="tpu_custom_call" | custom-call | flops 128849018880 | bytes 120000000 | tf_op jit(solution)/shard_map/backward/pallas_call | solution.py:395
  275.2 0.7 collective-permute-start.14
  275.9 1.4 collective-permute-start.15
  277.9 1.4 collective-permute-start.8
  279.3 20.8 %collective-permute-done.14.refs_1_ = bf16[3,128,1280]{2,1,0:T(8,128)(2,1)S(1)} collective-permute-done((bf16[3,128,1280]{2,1,0:T(8,128)(2,1)}, bf16[3,128,1280]{2,1,0:T(8,128)(2,1)S(1)}, u32[]{:S(2)}, u32[]{:S(2)}) %collective-permute-start.14) | collective-permute-done | bytes 983072 | tf_op jit(solution)/shard_map/ppermute | solution.py:468
  300.1 0.7 collective-permute-done.15.refs_2_
  300.7 1.4 collective-permute-start
  302.1 0.6 collective-permute-start.1
  302.7 18.4 %collective-permute-done.7.refs_1_ = bf16[3,128,1280]{2,1,0:T(8,128)(2,1)S(1)} collective-permute-done((bf16[3,128,1280]{2,1,0:T(8,128)(2,1)}, bf16[3,128,1280]{2,1,0:T(8,128)(2,1)S(1)}, u32[]{:S(2)}, u32[]{:S(2)}) %collective-permute-start.7) | collective-permute-done | bytes 983072 | tf_op jit(solution)/shard_map/ppermute | solution.py:468
  321.2 0.7 collective-permute-done.8.refs_2_
  321.8 1.4 collective-permute-start.16
  323.3 19.1 %collective-permute-done.refs_1_ = bf16[3,128,1280]{2,1,0:T(8,128)(2,1)} collective-permute-done((bf16[3,128,1280]{2,1,0:T(8,128)(2,1)}, bf16[3,128,1280]{2,1,0:T(8,128)(2,1)}, u32[]{:S(2)}, u32[]{:S(2)}) %collective-permute-start) | collective-permute-done | bytes 983072 | tf_op jit(solution)/shard_map/ppermute | solution.py:468
  342.4 9.8 %collective-permute-done.16.refs_3_ = bf16[3,128,1280]{2,1,0:T(8,128)(2,1)S(1)} collective-permute-done((bf16[3,128,1280]{2,1,0:T(8,128)(2,1)S(1)}, bf16[3,128,1280]{2,1,0:T(8,128)(2,1)S(1)}, u32[]{:S(2)}, u32[]{:S(2)}) %collective-permute-start.16) | collective-permute-done | bytes 983072 | tf_op jit(solution)/shard_map/ppermute | solution.py:468
  352.8 0.9 collective-permute-start.2
  353.6 9.2 %collective-permute-done.9.refs_3_ = bf16[3,128,1280]{2,1,0:T(8,128)(2,1)} collective-permute-done((bf16[3,128,1280]{2,1,0:T(8,128)(2,1)S(1)}, bf16[3,128,1280]{2,1,0:T(8,128)(2,1)}, u32[]{:S(2)}, u32[]{:S(2)}) %collective-permute-start.9) | collective-permute-done | bytes 983072 | tf_op jit(solution)/shard_map/ppermute | solution.py:468
  363.8 9.5 %collective-permute-done.2.refs_3_ = bf16[3,128,1280]{2,1,0:T(8,128)(2,1)} collective-permute-done((bf16[3,128,1280]{2,1,0:T(8,128)(2,1)}, bf16[3,128,1280]{2,1,0:T(8,128)(2,1)}, u32[]{:S(2)}, u32[]{:S(2)}) %collective-permute-start.2) | collective-permute-done | bytes 983072 | tf_op jit(solution)/shard_map/ppermute | solution.py:468
  374.1 0.8 copy-done.11
  374.9 16.9 %shard_map.180 = (bf16[2,1024,2560]{2,1,0:T(8,128)(2,1)}, bf16[2,1024,2560]{2,1,0:T(8,128)(2,1)}, bf16[2,2560,1024]{2,1,0:T(8,128)(2,1)}, f32[2,1024,2560]{2,1,0...) custom-call(s32[1]{0:T(128)} %bitcast.me_ref, ...), custom_call_target="tpu_custom_call" | custom-call | flops 393216000 | bytes 43253760 | tf_op jit(solution)/shard_map/pallas_call | solution.py:456
  391.7 16.9 %shard_map.181 = (bf16[2,1024,2560]{2,1,0:T(8,128)(2,1)}, bf16[2,1024,2560]{2,1,0:T(8,128)(2,1)}, bf16[2,2560,1024]{2,1,0:T(8,128)(2,1)}, f32[2,1024,2560]{2,1,0...) custom-call(s32[1]{0:T(128)} %bitcast.me_ref, ...), custom_call_target="tpu_custom_call", output_to_operand_aliasing={{0}: (19, {}), {1}: (20, {}), {2}: (21, {}), {3}: (22, {}),... | custom-call | flops 393216000 | bytes 43253760 | tf_op jit(solution)/shard_map/pallas_call | solution.py:456
  408.7 31.9 %shard_map.182 = (bf16[2,1024,2560]{2,1,0:T(8,128)(2,1)}, bf16[2,1024,2560]{2,1,0:T(8,128)(2,1)}, bf16[2,2560,1024]{2,1,0:T(8,128)(2,1)}, f32[2,1024,2560]{2,1,0...) custom-call(s32[1]{0:T(128)} %bitcast.me_ref, ...), custom_call_target="tpu_custom_call", output_to_operand_aliasing={{0}: (19, {}), {1}: (20, {}), {2}: (21, {}), {3}: (22, {}),... | custom-call | flops 786432000 | bytes 86507520 | tf_op jit(solution)/shard_map/pallas_call | solution.py:456
  440.6 31.9 %shard_map.183 = (bf16[2,1024,2560]{2,1,0:T(8,128)(2,1)}, bf16[2,1024,2560]{2,1,0:T(8,128)(2,1)}, bf16[2,2560,1024]{2,1,0:T(8,128)(2,1)}, f32[2,1024,2560]{2,1,0...) custom-call(s32[1]{0:T(128)} %bitcast.me_ref, ...), custom_call_target="tpu_custom_call", output_to_operand_aliasing={{0}: (19, {}), {1}: (20, {}), {2}: (21, {}), {3}: (22, {}),... | custom-call | flops 786432000 | bytes 86507520 | tf_op jit(solution)/shard_map/pallas_call | solution.py:456
  472.5 31.9 %shard_map.184 = (bf16[2,1024,2560]{2,1,0:T(8,128)(2,1)}, bf16[2,1024,2560]{2,1,0:T(8,128)(2,1)}, bf16[2,2560,1024]{2,1,0:T(8,128)(2,1)}, f32[2,1024,2560]{2,1,0...) custom-call(s32[1]{0:T(128)} %bitcast.me_ref, ...), custom_call_target="tpu_custom_call", output_to_operand_aliasing={{0}: (19, {}), {1}: (20, {}), {2}: (21, {}), {3}: (22, {}),... | custom-call | flops 786432000 | bytes 86507520 | tf_op jit(solution)/shard_map/pallas_call | solution.py:456
  (54 shorter events, 3.1 us)
Async XLA Ops:
  275.1 2.8 collective-permute-start.21
  275.2 24.8 %collective-permute-start.14 = (bf16[3,128,1280]{2,1,0:T(8,128)(2,1)}, bf16[3,128,1280]{2,1,0:T(8,128)(2,1)S(1)}, u32[]{:S(2)}, u32[]{:S(2)}) collective-permute-start(bf16[3,128,1280]{2,1,0:T(8,128)(2,1)} %get-tuple-element.70.refs_0_), channel_id=1, source_target_pairs={{0,2},{1,5},{2,0},{3,7},{4,6},{5,1},{6,4},{7,3}} | collective-permute-start | bytes 2949128 | tf_op jit(solution)/shard_map/ppermute | solution.py:468
  275.9 24.8 %collective-permute-start.15 = (bf16[3,128,1280]{2,1,0:T(8,128)(2,1)}, bf16[3,128,1280]{2,1,0:T(8,128)(2,1)S(1)}, u32[]{:S(2)}, u32[]{:S(2)}) collective-permute-start(bf16[3,128,1280]{2,1,0:T(8,128)(2,1)} %get-tuple-element.70.refs_0_), channel_id=1, source_target_pairs={{0,4},{1,3},{2,6},{3,1},{4,0},{5,7},{6,2},{7,5}} | collective-permute-start | bytes 2949128 | tf_op jit(solution)/shard_map/ppermute | solution.py:468
  277.3 24.8 %collective-permute-start.17 = (bf16[3,128,1280]{2,1,0:T(8,128)(2,1)}, bf16[3,128,1280]{2,1,0:T(8,128)(2,1)S(1)}, u32[]{:S(2)}, u32[]{:S(2)}) collective-permute-start(bf16[3,128,1280]{2,1,0:T(8,128)(2,1)} %get-tuple-element.70.refs_0_), channel_id=1, source_target_pairs={{0,1},{1,0},{2,3},{3,2},{4,5},{5,4},{6,7},{7,6}} | collective-permute-start | bytes 2949128 | tf_op jit(solution)/shard_map/ppermute | solution.py:468
  277.3 43.8 %collective-permute-start.7 = (bf16[3,128,1280]{2,1,0:T(8,128)(2,1)}, bf16[3,128,1280]{2,1,0:T(8,128)(2,1)S(1)}, u32[]{:S(2)}, u32[]{:S(2)}) collective-permute-start(bf16[3,128,1280]{2,1,0:T(8,128)(2,1)} %get-tuple-element.69.refs_0_), channel_id=1, source_target_pairs={{0,2},{1,5},{2,0},{3,7},{4,6},{5,1},{6,4},{7,3}} | collective-permute-start | bytes 2949128 | tf_op jit(solution)/shard_map/ppermute | solution.py:468
  277.9 97.0 %copy-start = (bf16[3,128,1280]{2,1,0:T(8,128)(2,1)}, bf16[3,128,1280]{2,1,0:T(8,128)(2,1)S(1)}, u32[]{:S(2)}) copy-start(bf16[3,128,1280]{2,1,0:T(8,128)(2,1)S(1)} %collective-permute-done.21.refs_4_) | copy-start | bytes 2949124
  277.9 43.9 %collective-permute-start.8 = (bf16[3,128,1280]{2,1,0:T(8,128)(2,1)}, bf16[3,128,1280]{2,1,0:T(8,128)(2,1)S(1)}, u32[]{:S(2)}, u32[]{:S(2)}) collective-permute-start(bf16[3,128,1280]{2,1,0:T(8,128)(2,1)} %get-tuple-element.69.refs_0_), channel_id=1, source_target_pairs={{0,4},{1,3},{2,6},{3,1},{4,0},{5,7},{6,2},{7,5}} | collective-permute-start | bytes 2949128 | tf_op jit(solution)/shard_map/ppermute | solution.py:468
  300.1 23.2 %collective-permute-start.10 = (bf16[3,128,1280]{2,1,0:T(8,128)(2,1)}, bf16[3,128,1280]{2,1,0:T(8,128)(2,1)S(1)}, u32[]{:S(2)}, u32[]{:S(2)}) collective-permute-start(bf16[3,128,1280]{2,1,0:T(8,128)(2,1)} %get-tuple-element.69.refs_0_), channel_id=1, source_target_pairs={{0,1},{1,0},{2,3},{3,2},{4,5},{5,4},{6,7},{7,6}} | collective-permute-start | bytes 2949128 | tf_op jit(solution)/shard_map/ppermute | solution.py:468
  300.7 41.6 %collective-permute-start = (bf16[3,128,1280]{2,1,0:T(8,128)(2,1)}, bf16[3,128,1280]{2,1,0:T(8,128)(2,1)}, u32[]{:S(2)}, u32[]{:S(2)}) collective-permute-start(bf16[3,128,1280]{2,1,0:T(8,128)(2,1)} %get-tuple-element.68.refs_0_), channel_id=1, source_target_pairs={{0,2},{1,5},{2,0},{3,7},{4,6},{5,1},{6,4},{7,3}} | collective-permute-start | bytes 2949128 | tf_op jit(solution)/shard_map/ppermute | solution.py:468
  302.1 40.2 %collective-permute-start.1 = (bf16[3,128,1280]{2,1,0:T(8,128)(2,1)}, bf16[3,128,1280]{2,1,0:T(8,128)(2,1)}, u32[]{:S(2)}, u32[]{:S(2)}) collective-permute-start(bf16[3,128,1280]{2,1,0:T(8,128)(2,1)} %get-tuple-element.68.refs_0_), channel_id=1, source_target_pairs={{0,4},{1,3},{2,6},{3,1},{4,0},{5,7},{6,2},{7,5}} | collective-permute-start | bytes 2949128 | tf_op jit(solution)/shard_map/ppermute | solution.py:468
  321.2 52.3 %collective-permute-start.22 = (bf16[3,3,128,1280]{3,2,1,0:T(8,128)(2,1)}, bf16[3,3,128,1280]{3,2,1,0:T(8,128)(2,1)}, u32[]{:S(2)}, u32[]{:S(2)}) collective-permute-start(bf16[3,3,128,1280]{3,2,1,0:T(8,128)(2,1)} %get-tuple-element.72.refs_1_.refs_2_.refs_3_), channel_id=1, source_target_pairs={{0,1},{1,0},{2,3},{3,2},{4,5},{5,4},{6,7},{7,6}} | collective-permute-start | bytes 8847368 | tf_op jit(solution)/shard_map/ppermute | solution.py:468
  321.8 30.4 %collective-permute-start.16 = (bf16[3,128,1280]{2,1,0:T(8,128)(2,1)S(1)}, bf16[3,128,1280]{2,1,0:T(8,128)(2,1)S(1)}, u32[]{:S(2)}, u32[]{:S(2)}) collective-permute-start(bf16[3,128,1280]{2,1,0:T(8,128)(2,1)S(1)} %collective-permute-done.14.refs_1_), channel_id=1, source_target_pairs={{0,4},{1,3},{2,6},{3,1},{4,0},{5,7},{6,2},{7,5}} | collective-permute-start | bytes 2949128 | tf_op jit(solution)/shard_map/ppermute | solution.py:468
  323.2 29.5 %collective-permute-start.18 = (bf16[3,128,1280]{2,1,0:T(8,128)(2,1)S(1)}, bf16[3,128,1280]{2,1,0:T(8,128)(2,1)}, u32[]{:S(2)}, u32[]{:S(2)}) collective-permute-start(bf16[3,128,1280]{2,1,0:T(8,128)(2,1)S(1)} %collective-permute-done.14.refs_1_), channel_id=1, source_target_pairs={{0,1},{1,0},{2,3},{3,2},{4,5},{5,4},{6,7},{7,6}} | collective-permute-start | bytes 2949128 | tf_op jit(solution)/shard_map/ppermute | solution.py:468
  342.3 10.4 %collective-permute-start.19 = (bf16[3,128,1280]{2,1,0:T(8,128)(2,1)S(1)}, bf16[3,128,1280]{2,1,0:T(8,128)(2,1)S(1)}, u32[]{:S(2)}, u32[]{:S(2)}) collective-permute-start(bf16[3,128,1280]{2,1,0:T(8,128)(2,1)S(1)} %collective-permute-done.15.refs_2_), channel_id=1, source_target_pairs={{0,1},{1,0},{2,3},{3,2},{4,5},{5,4},{6,7},{7,6}} | collective-permute-start | bytes 2949128 | tf_op jit(solution)/shard_map/ppermute | solution.py:468
  342.3 20.5 %collective-permute-start.9 = (bf16[3,128,1280]{2,1,0:T(8,128)(2,1)S(1)}, bf16[3,128,1280]{2,1,0:T(8,128)(2,1)}, u32[]{:S(2)}, u32[]{:S(2)}) collective-permute-start(bf16[3,128,1280]{2,1,0:T(8,128)(2,1)S(1)} %collective-permute-done.7.refs_1_), channel_id=1, source_target_pairs={{0,4},{1,3},{2,6},{3,1},{4,0},{5,7},{6,2},{7,5}} | collective-permute-start | bytes 2949128 | tf_op jit(solution)/shard_map/ppermute | solution.py:468
  352.2 11.1 %collective-permute-start.11 = (bf16[3,128,1280]{2,1,0:T(8,128)(2,1)S(1)}, bf16[3,128,1280]{2,1,0:T(8,128)(2,1)S(1)}, u32[]{:S(2)}, u32[]{:S(2)}) collective-permute-start(bf16[3,128,1280]{2,1,0:T(8,128)(2,1)S(1)} %collective-permute-done.7.refs_1_), channel_id=1, source_target_pairs={{0,1},{1,0},{2,3},{3,2},{4,5},{5,4},{6,7},{7,6}} | collective-permute-start | bytes 2949128 | tf_op jit(solution)/shard_map/ppermute | solution.py:468
  352.7 10.6 %collective-permute-start.12 = (bf16[3,128,1280]{2,1,0:T(8,128)(2,1)S(1)}, bf16[3,128,1280]{2,1,0:T(8,128)(2,1)S(1)}, u32[]{:S(2)}, u32[]{:S(2)}) collective-permute-start(bf16[3,128,1280]{2,1,0:T(8,128)(2,1)S(1)} %collective-permute-done.8.refs_2_), channel_id=1, source_target_pairs={{0,1},{1,0},{2,3},{3,2},{4,5},{5,4},{6,7},{7,6}} | collective-permute-start | bytes 2949128 | tf_op jit(solution)/shard_map/ppermute | solution.py:468
  352.8 20.6 %collective-permute-start.2 = (bf16[3,128,1280]{2,1,0:T(8,128)(2,1)}, bf16[3,128,1280]{2,1,0:T(8,128)(2,1)}, u32[]{:S(2)}, u32[]{:S(2)}) collective-permute-start(bf16[3,128,1280]{2,1,0:T(8,128)(2,1)} %collective-permute-done.refs_1_), channel_id=1, source_target_pairs={{0,4},{1,3},{2,6},{3,1},{4,0},{5,7},{6,2},{7,5}} | collective-permute-start | bytes 2949128 | tf_op jit(solution)/shard_map/ppermute | solution.py:468
  362.8 11.1 %collective-permute-start.20 = (bf16[3,128,1280]{2,1,0:T(8,128)(2,1)S(1)}, bf16[3,128,1280]{2,1,0:T(8,128)(2,1)S(1)}, u32[]{:S(2)}, u32[]{:S(2)}) collective-permute-start(bf16[3,128,1280]{2,1,0:T(8,128)(2,1)S(1)} %collective-permute-done.16.refs_3_), channel_id=1, source_target_pairs={{0,1},{1,0},{2,3},{3,2},{4,5},{5,4},{6,7},{7,6}} | collective-permute-start | bytes 2949128 | tf_op jit(solution)/shard_map/ppermute | solution.py:468
  363.3 77.3 %collective-permute-start.13 = (bf16[3,128,1280]{2,1,0:T(8,128)(2,1)}, bf16[3,128,1280]{2,1,0:T(8,128)(2,1)}, u32[]{:S(2)}, u32[]{:S(2)}) collective-permute-start(bf16[3,128,1280]{2,1,0:T(8,128)(2,1)} %collective-permute-done.9.refs_3_), channel_id=1, source_target_pairs={{0,1},{1,0},{2,3},{3,2},{4,5},{5,4},{6,7},{7,6}} | collective-permute-start | bytes 2949128 | tf_op jit(solution)/shard_map/ppermute | solution.py:468
  363.4 109.2 %collective-permute-start.3 = (bf16[3,128,1280]{2,1,0:T(8,128)(2,1)}, bf16[3,128,1280]{2,1,0:T(8,128)(2,1)}, u32[]{:S(2)}, u32[]{:S(2)}) collective-permute-start(bf16[3,128,1280]{2,1,0:T(8,128)(2,1)} %get-tuple-element.68.refs_0_), channel_id=1, source_target_pairs={{0,1},{1,0},{2,3},{3,2},{4,5},{5,4},{6,7},{7,6}} | collective-permute-start | bytes 2949128 | tf_op jit(solution)/shard_map/ppermute | solution.py:468
  373.3 99.2 %collective-permute-start.4 = (bf16[3,128,1280]{2,1,0:T(8,128)(2,1)}, bf16[3,128,1280]{2,1,0:T(8,128)(2,1)}, u32[]{:S(2)}, u32[]{:S(2)}) collective-permute-start(bf16[3,128,1280]{2,1,0:T(8,128)(2,1)} %collective-permute-done.refs_1_), channel_id=1, source_target_pairs={{0,1},{1,0},{2,3},{3,2},{4,5},{5,4},{6,7},{7,6}} | collective-permute-start | bytes 2949128 | tf_op jit(solution)/shard_map/ppermute | solution.py:468
  373.5 99.0 %collective-permute-start.5 = (bf16[3,128,1280]{2,1,0:T(8,128)(2,1)}, bf16[3,128,1280]{2,1,0:T(8,128)(2,1)}, u32[]{:S(2)}, u32[]{:S(2)}) collective-permute-start(bf16[3,128,1280]{2,1,0:T(8,128)(2,1)} %collective-permute-done.1.refs_2_), channel_id=1, source_target_pairs={{0,1},{1,0},{2,3},{3,2},{4,5},{5,4},{6,7},{7,6}} | collective-permute-start | bytes 2949128 | tf_op jit(solution)/shard_map/ppermute | solution.py:468
  373.9 98.6 %collective-permute-start.6 = (bf16[3,128,1280]{2,1,0:T(8,128)(2,1)}, bf16[3,128,1280]{2,1,0:T(8,128)(2,1)}, u32[]{:S(2)}, u32[]{:S(2)}) collective-permute-start(bf16[3,128,1280]{2,1,0:T(8,128)(2,1)} %collective-permute-done.2.refs_3_), channel_id=1, source_target_pairs={{0,1},{1,0},{2,3},{3,2},{4,5},{5,4},{6,7},{7,6}} | collective-permute-start | bytes 2949128 | tf_op jit(solution)/shard_map/ppermute | solution.py:468
  (11 other events, 385.1 us)

commit v3 on v2

--- a/solution.py
+++ b/solution.py
@@ -73,57 +73,72 @@
 MM = 2 * T * D * F
 
 
-def gate_up(me, x, w_gate, w_up):
-    def kernel(me_ref, x_ref, wg_ref, wu_ref, g_ref, u_ref, act_ref, a_ref):
-        @pl.when(pl.program_id(0) == 0)
+def forward(me, x, dy, w_gate, w_up, w_down):
+    n, rows = F // FT, T // 8
+
+    def kernel(me_ref, x_ref, dy_ref, wg_ref, wu_ref, wd_ref, g_ref, u_ref, out_ref, a1_ref, a1t_ref, a0t_ref, dyt_ref, a_ref, acc_ref):
+        j = pl.program_id(0)
+
+        @pl.when(j == 0)
         def _():
             for t in range(T // SUB):
-                rows = slice(t * SUB, (t + 1) * SUB)
-                a_ref[rows, :] = normed(x_ref[rows, :])
-
-        for t in range(T // SUB):
-            rows = slice(t * SUB, (t + 1) * SUB)
-            g = dot(a_ref[rows], wg_ref[0])
-            u = dot(a_ref[rows], wu_ref[0])
-            g_ref[rows, :] = g
-            u_ref[rows, :] = u
-            act_ref[rows, :] = (g * sigmoid(g) * u).astype(BF16)
-
-    weight = pl.BlockSpec((1, D, FT), lambda j, m: (0, 0, j))
-    tile = pl.BlockSpec((T, FT), lambda j, m: (0, j))
+                here = slice(t * SUB, (t + 1) * SUB)
+                a_ref[here, :] = normed(x_ref[here, :])
+
+        def tile(first):
+            for t in range(T // SUB):
+                here = slice(t * SUB, (t + 1) * SUB)
+                g = dot(a_ref[here], wg_ref[0])
+                u = dot(a_ref[here], wu_ref[0])
+                g_ref[here, :] = g
+                u_ref[here, :] = u
+                more = dot((g * sigmoid(g) * u).astype(BF16), wd_ref[0])
+                acc_ref[here, :] = more if first else acc_ref[here, :] + more
+            chunk = pl.ds(pl.multiple_of(jnp.minimum(j, 7) * rows, rows), rows)
+            store_turned(me_ref[0], a_ref[chunk, :], a0t_ref)
+            store_turned(me_ref[0], dy_ref[...], dyt_ref)
+
+        @pl.when(j == 0)
+        def _():
+            tile(True)
+
+        @pl.when((j > 0) & (j < n))
+        def _():
+            tile(False)
+
+        @pl.when(j >= n)
+        def _():
+            here = pl.ds(pl.multiple_of((j - n) * SUB, SUB), SUB)
+            out = x_ref[here, :] + acc_ref[here, :].astype(BF16)
+            out_ref[...] = out
+            a = normed(out)
+            a1_ref[...] = a
+            store_turned(me_ref[0], a, a1t_ref)
+
+    tile = lambda j: jnp.minimum(j, n - 1)
+    row = lambda j: jnp.maximum(j - n, 0)
+    part = lambda j: jnp.minimum(j, 7)
+    weight = pl.BlockSpec((1, D, FT), lambda j, m: (0, 0, tile(j)))
+    kept = pl.BlockSpec((T, FT), lambda j, m: (0, tile(j)))
+    tall = pl.BlockSpec((SUB, D), lambda j, m: (row(j), 0))
+    flat = pl.BlockSpec((D, rows), lambda j, m: (0, part(j)))
     return call(
         kernel,
-        (F // FT,),
-        [pl.BlockSpec((T, D), lambda j, m: (0, 0), pipeline_mode=pl.Buffered(1)), weight, weight],
-        [(tile, shaped((T, F), F32)), (tile, shaped((T, F), F32)), (tile, shaped((T, F)))],
-        [pltpu.VMEM((T, D), BF16)],
-        flops=2 * MM,
-        moved=67e6,
-    )(me, x, w_gate, w_up)
-
-
-def down(me, act, w_down, x, dy):
-    rows = 512
-
-    def kernel(me_ref, act_ref, wd_ref, x_ref, dy_ref, out_ref, a_ref, at_ref, a0t_ref, dyt_ref):
-        store_turned(me_ref[0], normed(x_ref[...]), a0t_ref)
-        store_turned(me_ref[0], dy_ref[...], dyt_ref)
-        out = x_ref[...] + dot(act_ref[...], wd_ref[0]).astype(BF16)
-        out_ref[...] = out
-        a = normed(out)
-        a_ref[...] = a
-        store_turned(me_ref[0], a, at_ref)
-
-    tall = pl.BlockSpec((rows, D), lambda i, m: (i, 0))
-    flat = pl.BlockSpec((D, rows), lambda i, m: (0, i))
-    return call(
-        kernel,
-        (T // rows,),
-        [pl.BlockSpec((rows, F), lambda i, m: (i, 0)), pl.BlockSpec((1, F, D), lambda i, m: (0, 0, 0), pipeline_mode=pl.Buffered(1)), tall, tall],
-        [(tall, shaped((T, D))), (tall, shaped((T, D)))] + [(flat, shaped((D, T)))] * 3,
-        flops=MM,
-        moved=44e6,
-    )(me, act, w_down, x, dy)
+        (n + T // SUB,),
+        [
+            pl.BlockSpec((T, D), lambda j, m: (0, 0), pipeline_mode=pl.Buffered(1)),
+            pl.BlockSpec((rows, D), lambda j, m: (part(j), 0)),
+            weight,
+            weight,
+            pl.BlockSpec((1, FT, D), lambda j, m: (0, tile(j), 0)),
+        ],
+        [(kept, shaped((T, F), F32))] * 2
+        + [(tall, shaped((T, D)))] * 2
+        + [(pl.BlockSpec((D, SUB), lambda j, m: (0, row(j))), shaped((D, T))), (flat, shaped((D, T))), (flat, shaped((D, T)))],
+        [pltpu.VMEM((T, D), BF16), pltpu.VMEM((T, D), F32)],
+        flops=3 * MM,
+        moved=90e6,
+    )(me, x, dy, w_gate, w_up, w_down)
 
 
 def both(a, b):
@@ -143,12 +158,12 @@
         dy_ref, a1_ref, a1t_ref, dyt_ref, h_ref, a0t_ref = take(6)
         wd_ref, wg_ref, wu_ref, g_ref, u_ref = take(5)
         owns = take(4)
-        got_ref, factor_ref = take(2)
+        got_ref, over_ref, factor_ref = take(3)
         dg_ref, du_ref, act_ref = take(3)
         dh_v, a_v, at_v, dht_v, acc = take(5)
         keep, send, recv0, away1, stay1, recv1, away2, stay2, recv2, own_v = take(10)
         sq_ref, all_sq = take(2)
-        sems, s0, r0, s1, r1, s2, r2, s3, r3, s4, r4, s5, r5, s6, r6 = take(15)
+        sems, s0, r0, s1, r1, s2, r2, s3, r3, s4, r4, s5, r5, s6, r6, s7, r7 = take(17)
         pairs = ((dy_ref, dh_v), (a1_ref, a_v), (a1t_ref, at_v), (dyt_ref, dht_v), (h_ref, a_v), (a0t_ref, at_v))
         copies = [pltpu.make_async_copy(s, d, sems.at[i]) for i, (s, d) in enumerate(pairs)]
         j = pl.program_id(0)
@@ -179,6 +194,10 @@
         def gather_near(t):
             return (remote(own_v.at[t], place_of(2, t), s4.at[t], r4.at[t], near), remote(place_of(1, t), place_of(3, t), s5.at[t], r5.at[t], near))
 
+        def core_swaps():
+            tiles = [remote(own_v.at[t], over_ref.at[0, :, :, pl.ds(t * FT, FT)], s7.at[t], r7.at[t], other) for t in range(mid)]
+            return tiles + [remote(got_ref, over_ref.at[pl.ds(1, 3)], s7.at[mid], r7.at[mid], other)]
+
         def tell(o):
             return remote(sq_ref, all_sq.at[me], s6.at[o - 1], r6.at[me], (me + o) % 8)
 
@@ -190,6 +209,15 @@
 
         def behind(steps):
             return between(steps, n) | between(low + steps, n)
+
+        def two_speeds(steps, slower, work):
+            @pl.when(between(steps, n))
+            def _():
+                work(j - steps)
+
+            @pl.when(between(low + slower, n))
+            def _():
+                work(j - slower)
 
         barrier = pltpu.get_barrier_semaphore()
 
@@ -201,17 +229,22 @@
                 c.start()
             sq_ref[...] = jnp.zeros_like(sq_ref)
 
-        @pl.when(between(10, mid))
-        def _():
-            for c in gather_near(j - 10):
+        @pl.when(between(8, mid))
+        def _():
+            for c in gather_near(j - 8):
                 c.wait()
 
-        @pl.when(between(8, mid))
-        def _():
-            gather_far(j - 8).wait()
+        @pl.when(between(6, mid))
+        def _():
+            gather_far(j - 6).wait()
+
+        @pl.when(j == 16)
+        def _():
+            for c in core_swaps():
+                c.wait()
 
         def finish(out, number):
-            t = j - 6
+            t = j - (4 if number < 2 else 6)
             far_copy(t).wait()
             for i in range(3):
                 done = both(stay2[t % 2, i], recv2[t % 5, i])
@@ -224,17 +257,17 @@
 
         for number, first in enumerate((0, mid, low, low + mid)):
 
-            @pl.when(between(first + 6, mid))
+            @pl.when(between(first + (4 if number < 2 else 6), mid))
             def _(number=number):
                 finish(owns[number], number)
 
-        @pl.when(behind(4))
-        def _():
-            t = j - 4
+        def second_sum(t):
             near_copy(t).wait()
             for i in range(3):
                 away2[t % 2, i] = both(stay1[t % 2, 1, i], recv1[t % 5, 1, i])
                 stay2[t % 2, i] = both(stay1[t % 2, 0, i], recv1[t % 5, 0, i])
+
+        two_speeds(3, 4, second_sum)
 
         @pl.when(behind(2))
         def _():
@@ -315,9 +348,7 @@
             factor = jnp.minimum(1.0, 0.5 * lax.rsqrt(total / (3 * L * D * F) + 1e-30))
             factor_ref[...] = jnp.broadcast_to(factor, (8, 128))
 
-        @pl.when(behind(4))
-        def _():
-            far_copy(j - 4).start()
+        two_speeds(3, 4, lambda t: far_copy(t).start())
 
         @pl.when(behind(2))
         def _():
@@ -327,13 +358,18 @@
         def _():
             core_copy(j - 1).start()
 
+        @pl.when(between(4, mid))
+        def _():
+            gather_far(j - 4).start()
+
+        @pl.when(j == 13)
+        def _():
+            for c in core_swaps():
+                c.start()
+
         @pl.when(between(6, mid))
         def _():
-            gather_far(j - 6).start()
-
-        @pl.when(between(8, mid))
-        def _():
-            for c in gather_near(j - 8):
+            for c in gather_near(j - 6):
                 c.start()
 
         work(range(1, T // SUB))
@@ -381,17 +417,17 @@
     tile = pl.BlockSpec((T, FT), lambda j: (0, lower(j)))
 
     def shard(first):
-        return pl.BlockSpec((3, BLK, FT), lambda j: (0, 0, jnp.clip(j - 6 - first, 0, mid - 1))), shaped((3, BLK, WIDE))
-
-    outs = [shard(first) for first in (0, mid, low, low + mid)]
-    outs += [(whole, shaped((3, 3, BLK, WIDE))), (pl.BlockSpec((8, 128), lambda j: (0, 0)), shaped((8, 128), F32))]
+        return pl.BlockSpec((3, BLK, FT), lambda j: (0, 0, jnp.clip(j - first, 0, mid - 1))), shaped((3, BLK, WIDE))
+
+    outs = [shard(first) for first in (4, 4 + mid, low + 6, low + 6 + mid)]
+    outs += [(whole, shaped((3, 3, BLK, WIDE))), (whole, shaped((4, 3, BLK, WIDE))), (pl.BlockSpec((8, 128), lambda j: (0, 0)), shaped((8, 128), F32))]
     sem = pltpu.SemaphoreType.DMA
     quarter = lambda *lead: pltpu.VMEM((*lead, 3, BLK, FT), BF16)
     scratch = [pltpu.VMEM((T, FT), BF16)] * 3
     scratch += [pltpu.VMEM((T, D), BF16)] * 2 + [pltpu.VMEM((D, T), BF16)] * 2 + [pltpu.VMEM((T, D), F32)]
     scratch += [quarter(2, 4), quarter(2, 4), quarter(3, 4), quarter(2, 2), quarter(2, 2), quarter(5, 2), quarter(2), quarter(2), quarter(5), quarter(mid)]
     scratch += [pltpu.VMEM((8, 128), F32), pltpu.VMEM((8, 8, 128), F32)]
-    scratch += [sem((k,)) for k in (6, 2, 3, 2, 5, 2, 5, mid, mid, mid, mid, mid, mid, 7, 8)]
+    scratch += [sem((k,)) for k in (6, 2, 3, 2, 5, 2, 5, mid, mid, mid, mid, mid, mid, 7, 8, mid + 1, mid + 1)]
     return pl.pallas_call(
         kernel,
         grid_spec=pltpu.PrefetchScalarGridSpec(
@@ -405,7 +441,7 @@
 
 
 def adamw(me, layer, first, width, base, factor, parts, w, m, v, so_far):
-    ft = 640
+    ft = width
     steps, at0, part0 = width // ft, first // ft, (first - base) // ft
 
     def kernel(me_ref, f_ref, *refs):
@@ -480,13 +516,10 @@
         w_gate, w_up, w_down = weights
         x, dy = x[0], dy[0]
         me = lax.axis_index("dp").astype(jnp.int32).reshape(1)
-        gate, up, act = gate_up(me, x, w_gate, w_up)
-        h, a1, a1t, a0t, dyt = down(me, act, w_down, x, dy)
-        own1a, own1b, own0a, own0b, got, factor = backward(dy, a1, a1t, dyt, h, a0t, gate, up, *weights)
-
-        parts = [(own1a, None)] + [(got, k) for k in range(3)]
-        across = swap(own1a, "core"), swap(got, "core")
-        parts += [(across[0], None)] + [(across[1], k) for k in range(3)]
+        gate, up, h, a1, a1t, a0t, dyt = forward(me, x, dy, *weights)
+        own1a, own1b, own0a, own0b, got, over, factor = backward(dy, a1, a1t, dyt, h, a0t, gate, up, *weights)
+
+        parts = [(own1a, None)] + [(got, k) for k in range(3)] + [(over, k) for k in range(4)]
         new = None
         for first in (0, WIDE // 2):
             new = adamw(me, 1, first, WIDE // 2, 0, factor, parts, weights, m, v, new)

time: 506 us -> 491 us (0.970)
  Pallas kernels: 404 us -> 390 us
    pallas_call x5, Pallas kernels: 129 us -> 119 us  [adamw(): call(kernel, (8, steps), ins, outs, [pltpu.VMEM((3, BLK, ft), BF16)], flo...]
    pallas_call x2 -> x1, Pallas kernels: 52.7 us -> 47.6 us  [forward(): call(kernel, (n + T // SUB,), [pl.BlockSpec((T, D), lambda j, m: (0, 0),...]
    ppermute x23 -> x21, waiting for transfers between devices: 88.2 us -> 84.5 us  [swap(): return lax.ppermute(a, 'dp', STAGES[stage])]
    ppermute x23 -> x21, starting transfers between devices: 10.7 us -> 14 us  [swap(): return lax.ppermute(a, 'dp', STAGES[stage])]
  transfers between devices with their start and end apart: 23 -> 21, of which waited for: 8 -> 7; matrix products, arithmetic and copies ran while one was open for 0% -> 0% of each run, Pallas kernels for 19% -> 19%
where the time goes in v3:
time: 491 us
  Pallas kernels  390 us (79%)
  waiting for transfers between devices  84.5 us (17%)
  starting transfers between devices  14 us (3%)
    pallas_call x1, Pallas kernels, backward(): pl.pallas_call(kernel, grid_spec=pltpu.PrefetchScalarGridSpec(num_scalar_...  223 us
    pallas_call x5, Pallas kernels, adamw(): call(kernel, (8, steps), ins, outs, [pltpu.VMEM((3, BLK, ft), BF16)], flo...  119 us
    ppermute x21, waiting for transfers between devices, swap(): return lax.ppermute(a, 'dp', STAGES[stage])  84.5 us
    pallas_call x1, Pallas kernels, forward(): call(kernel, (n + T // SUB,), [pl.BlockSpec((T, D), lambda j, m: (0, 0),...  47.6 us
    ppermute x21, starting transfers between devices, swap(): return lax.ppermute(a, 'dp', STAGES[stage])  14 us
  transfers between devices with their start and end apart: 21, of which 7 were waited for; matrix products, arithmetic and copies ran while one was open for 0% of the time, Pallas kernels for 19%

profile of v3, /device:TPU:0, one launch (start us, length us, event | category | flops | bytes accessed | tf_op | source)
XLA Modules:
  0.0 490.5 jit_solution(8600302324149385825)
XLA Ops:
  0.6 47.6 %shard_map.178 = (f32[2048,2560]{1,0:T(8,128)}, f32[2048,2560]{1,0:T(8,128)}, bf16[2048,1024]{1,0:T(8,128)(2,1)}, bf16[2048,1024]{1,0:T(8,128)(2,1)}, bf16[1024,...) custom-call(s32[1]{0:T(128)} %bitcast.me_ref, bf16[2048,1024]{1,0:T(8,128)(2,1)} %bitcast.3, ...), custom_call_target="tpu_custom_call" | custom-call | flops 32212254720 | bytes 90000000 | tf_op jit(solution)/shard_map/pallas_call | solution.py:125
  48.3 223.1 %backward.1 = (bf16[3,128,1280]{2,1,0:T(8,128)(2,1)}, bf16[3,128,1280]{2,1,0:T(8,128)(2,1)}, bf16[3,128,1280]{2,1,0:T(8,128)(2,1)}, bf16[3,128,1280]{2,1,0:T(8,1...) custom-call(bf16[2048,1024]{1,0:T(8,128)(2,1)} %bitcast.5, ...), custom_call_target="tpu_custom_call" | custom-call | flops 128849018880 | bytes 120000000 | tf_op jit(solution)/shard_map/backward/pallas_call | solution.py:431
  271.4 0.9 collective-permute-start.14
  272.3 1.0 collective-permute-start.15
  273.4 1.4 collective-permute-start.7
  275.5 20.6 %collective-permute-done.14.refs_1_ = bf16[3,128,1280]{2,1,0:T(8,128)(2,1)S(1)} collective-permute-done((bf16[3,128,1280]{2,1,0:T(8,128)(2,1)}, bf16[3,128,1280]{2,1,0:T(8,128)(2,1)S(1)}, u32[]{:S(2)}, u32[]{:S(2)}) %collective-permute-start.14) | collective-permute-done | bytes 983072 | tf_op jit(solution)/shard_map/ppermute | solution.py:504
  296.1 1.0 collective-permute-done.15.refs_2_
  297.1 1.1 collective-permute-start
  298.3 1.3 collective-permute-start.1
  299.6 17.6 %collective-permute-done.7.refs_1_ = bf16[3,128,1280]{2,1,0:T(8,128)(2,1)S(1)} collective-permute-done((bf16[3,128,1280]{2,1,0:T(8,128)(2,1)}, bf16[3,128,1280]{2,1,0:T(8,128)(2,1)S(1)}, u32[]{:S(2)}, u32[]{:S(2)}) %collective-permute-start.7) | collective-permute-done | bytes 983072 | tf_op jit(solution)/shard_map/ppermute | solution.py:504
  317.2 1.4 collective-permute-start.16
  319.1 19.2 %collective-permute-done.refs_1_ = bf16[3,128,1280]{2,1,0:T(8,128)(2,1)} collective-permute-done((bf16[3,128,1280]{2,1,0:T(8,128)(2,1)}, bf16[3,128,1280]{2,1,0:T(8,128)(2,1)}, u32[]{:S(2)}, u32[]{:S(2)}) %collective-permute-start) | collective-permute-done | bytes 983072 | tf_op jit(solution)/shard_map/ppermute | solution.py:504
  338.4 1.4 collective-permute-start.9
  339.8 8.3 %collective-permute-done.16.refs_3_ = bf16[3,128,1280]{2,1,0:T(8,128)(2,1)S(1)} collective-permute-done((bf16[3,128,1280]{2,1,0:T(8,128)(2,1)S(1)}, bf16[3,128,1280]{2,1,0:T(8,128)(2,1)S(1)}, u32[]{:S(2)}, u32[]{:S(2)}) %collective-permute-start.16) | collective-permute-done | bytes 983072 | tf_op jit(solution)/shard_map/ppermute | solution.py:504
  348.1 1.1 collective-permute-start.12
  350.1 8.7 %collective-permute-done.9.refs_3_ = bf16[3,128,1280]{2,1,0:T(8,128)(2,1)} collective-permute-done((bf16[3,128,1280]{2,1,0:T(8,128)(2,1)S(1)}, bf16[3,128,1280]{2,1,0:T(8,128)(2,1)}, u32[]{:S(2)}, u32[]{:S(2)}) %collective-permute-start.9) | collective-permute-done | bytes 983072 | tf_op jit(solution)/shard_map/ppermute | solution.py:504
  358.7 1.0 collective-permute-start.13
  360.2 9.0 %collective-permute-done.2.refs_3_ = bf16[3,128,1280]{2,1,0:T(8,128)(2,1)} collective-permute-done((bf16[3,128,1280]{2,1,0:T(8,128)(2,1)}, bf16[3,128,1280]{2,1,0:T(8,128)(2,1)}, u32[]{:S(2)}, u32[]{:S(2)}) %collective-permute-start.2) | collective-permute-done | bytes 983072 | tf_op jit(solution)/shard_map/ppermute | solution.py:504
  370.0 0.9 copy-done.11
  370.9 16.9 %shard_map.179 = (bf16[2,1024,2560]{2,1,0:T(8,128)(2,1)}, bf16[2,1024,2560]{2,1,0:T(8,128)(2,1)}, bf16[2,2560,1024]{2,1,0:T(8,128)(2,1)}, f32[2,1024,2560]{2,1,0...) custom-call(s32[1]{0:T(128)} %bitcast.me_ref, ...), custom_call_target="tpu_custom_call" | custom-call | flops 393216000 | bytes 43253760 | tf_op jit(solution)/shard_map/pallas_call | solution.py:492
  387.8 17.0 %shard_map.180 = (bf16[2,1024,2560]{2,1,0:T(8,128)(2,1)}, bf16[2,1024,2560]{2,1,0:T(8,128)(2,1)}, bf16[2,2560,1024]{2,1,0:T(8,128)(2,1)}, f32[2,1024,2560]{2,1,0...) custom-call(s32[1]{0:T(128)} %bitcast.me_ref, ...), custom_call_target="tpu_custom_call", output_to_operand_aliasing={{0}: (19, {}), {1}: (20, {}), {2}: (21, {}), {3}: (22, {}),... | custom-call | flops 393216000 | bytes 43253760 | tf_op jit(solution)/shard_map/pallas_call | solution.py:492
  404.8 28.4 %shard_map.181 = (bf16[2,1024,2560]{2,1,0:T(8,128)(2,1)}, bf16[2,1024,2560]{2,1,0:T(8,128)(2,1)}, bf16[2,2560,1024]{2,1,0:T(8,128)(2,1)}, f32[2,1024,2560]{2,1,0...) custom-call(s32[1]{0:T(128)} %bitcast.me_ref, ...), custom_call_target="tpu_custom_call", output_to_operand_aliasing={{0}: (19, {}), {1}: (20, {}), {2}: (21, {}), {3}: (22, {}),... | custom-call | flops 786432000 | bytes 86507520 | tf_op jit(solution)/shard_map/pallas_call | solution.py:492
  433.3 28.6 %shard_map.182 = (bf16[2,1024,2560]{2,1,0:T(8,128)(2,1)}, bf16[2,1024,2560]{2,1,0:T(8,128)(2,1)}, bf16[2,2560,1024]{2,1,0:T(8,128)(2,1)}, f32[2,1024,2560]{2,1,0...) custom-call(s32[1]{0:T(128)} %bitcast.me_ref, ...), custom_call_target="tpu_custom_call", output_to_operand_aliasing={{0}: (19, {}), {1}: (20, {}), {2}: (21, {}), {3}: (22, {}),... | custom-call | flops 786432000 | bytes 86507520 | tf_op jit(solution)/shard_map/pallas_call | solution.py:492
  461.9 28.4 %shard_map.183 = (bf16[2,1024,2560]{2,1,0:T(8,128)(2,1)}, bf16[2,1024,2560]{2,1,0:T(8,128)(2,1)}, bf16[2,2560,1024]{2,1,0:T(8,128)(2,1)}, f32[2,1024,2560]{2,1,0...) custom-call(s32[1]{0:T(128)} %bitcast.me_ref, ...), custom_call_target="tpu_custom_call", output_to_operand_aliasing={{0}: (19, {}), {1}: (20, {}), {2}: (21, {}), {3}: (22, {}),... | custom-call | flops 786432000 | bytes 86507520 | tf_op jit(solution)/shard_map/pallas_call | solution.py:492
  (49 shorter events, 3.5 us)
Async XLA Ops:
  271.4 24.7 %collective-permute-start.14 = (bf16[3,128,1280]{2,1,0:T(8,128)(2,1)}, bf16[3,128,1280]{2,1,0:T(8,128)(2,1)S(1)}, u32[]{:S(2)}, u32[]{:S(2)}) collective-permute-start(bf16[3,128,1280]{2,1,0:T(8,128)(2,1)} %get-tuple-element.69.refs_0_), channel_id=1, source_target_pairs={{0,2},{1,5},{2,0},{3,7},{4,6},{5,1},{6,4},{7,3}} | collective-permute-start | bytes 2949128 | tf_op jit(solution)/shard_map/ppermute | solution.py:504
  272.3 24.8 %collective-permute-start.15 = (bf16[3,128,1280]{2,1,0:T(8,128)(2,1)}, bf16[3,128,1280]{2,1,0:T(8,128)(2,1)S(1)}, u32[]{:S(2)}, u32[]{:S(2)}) collective-permute-start(bf16[3,128,1280]{2,1,0:T(8,128)(2,1)} %get-tuple-element.69.refs_0_), channel_id=1, source_target_pairs={{0,4},{1,3},{2,6},{3,1},{4,0},{5,7},{6,2},{7,5}} | collective-permute-start | bytes 2949128 | tf_op jit(solution)/shard_map/ppermute | solution.py:504
  273.4 24.9 %collective-permute-start.17 = (bf16[3,128,1280]{2,1,0:T(8,128)(2,1)}, bf16[3,128,1280]{2,1,0:T(8,128)(2,1)S(1)}, u32[]{:S(2)}, u32[]{:S(2)}) collective-permute-start(bf16[3,128,1280]{2,1,0:T(8,128)(2,1)} %get-tuple-element.69.refs_0_), channel_id=1, source_target_pairs={{0,1},{1,0},{2,3},{3,2},{4,5},{5,4},{6,7},{7,6}} | collective-permute-start | bytes 2949128 | tf_op jit(solution)/shard_map/ppermute | solution.py:504
  273.4 43.8 %collective-permute-start.7 = (bf16[3,128,1280]{2,1,0:T(8,128)(2,1)}, bf16[3,128,1280]{2,1,0:T(8,128)(2,1)S(1)}, u32[]{:S(2)}, u32[]{:S(2)}) collective-permute-start(bf16[3,128,1280]{2,1,0:T(8,128)(2,1)} %get-tuple-element.68.refs_0_), channel_id=1, source_target_pairs={{0,2},{1,5},{2,0},{3,7},{4,6},{5,1},{6,4},{7,3}} | collective-permute-start | bytes 2949128 | tf_op jit(solution)/shard_map/ppermute | solution.py:504
  274.7 43.9 %collective-permute-start.8 = (bf16[3,128,1280]{2,1,0:T(8,128)(2,1)}, bf16[3,128,1280]{2,1,0:T(8,128)(2,1)S(1)}, u32[]{:S(2)}, u32[]{:S(2)}) collective-permute-start(bf16[3,128,1280]{2,1,0:T(8,128)(2,1)} %get-tuple-element.68.refs_0_), channel_id=1, source_target_pairs={{0,4},{1,3},{2,6},{3,1},{4,0},{5,7},{6,2},{7,5}} | collective-permute-start | bytes 2949128 | tf_op jit(solution)/shard_map/ppermute | solution.py:504
  296.1 91.7 %copy-start.3 = (bf16[3,128,1280]{2,1,0:T(8,128)(2,1)}, bf16[3,128,1280]{2,1,0:T(8,128)(2,1)S(1)}, u32[]{:S(2)}) copy-start(bf16[3,128,1280]{2,1,0:T(8,128)(2,1)S(1)} %collective-permute-done.14.refs_1_) | copy-start | bytes 2949124
  296.1 22.5 %collective-permute-start.10 = (bf16[3,128,1280]{2,1,0:T(8,128)(2,1)}, bf16[3,128,1280]{2,1,0:T(8,128)(2,1)S(1)}, u32[]{:S(2)}, u32[]{:S(2)}) collective-permute-start(bf16[3,128,1280]{2,1,0:T(8,128)(2,1)} %get-tuple-element.68.refs_0_), channel_id=1, source_target_pairs={{0,1},{1,0},{2,3},{3,2},{4,5},{5,4},{6,7},{7,6}} | collective-permute-start | bytes 2949128 | tf_op jit(solution)/shard_map/ppermute | solution.py:504
  297.1 63.1 %copy-start.4 = (bf16[3,128,1280]{2,1,0:T(8,128)(2,1)}, bf16[3,128,1280]{2,1,0:T(8,128)(2,1)S(1)}, u32[]{:S(2)}) copy-start(bf16[3,128,1280]{2,1,0:T(8,128)(2,1)S(1)} %collective-permute-done.15.refs_2_) | copy-start | bytes 2949124
  297.1 41.2 %collective-permute-start = (bf16[3,128,1280]{2,1,0:T(8,128)(2,1)}, bf16[3,128,1280]{2,1,0:T(8,128)(2,1)}, u32[]{:S(2)}, u32[]{:S(2)}) collective-permute-start(bf16[3,128,1280]{2,1,0:T(8,128)(2,1)} %get-tuple-element.67.refs_0_), channel_id=1, source_target_pairs={{0,2},{1,5},{2,0},{3,7},{4,6},{5,1},{6,4},{7,3}} | collective-permute-start | bytes 2949128 | tf_op jit(solution)/shard_map/ppermute | solution.py:504
  298.3 71.0 %copy-start.5 = (bf16[3,128,1280]{2,1,0:T(8,128)(2,1)}, bf16[3,128,1280]{2,1,0:T(8,128)(2,1)S(1)}, u32[]{:S(2)}) copy-start(bf16[3,128,1280]{2,1,0:T(8,128)(2,1)S(1)} %collective-permute-done.17.refs_4_) | copy-start | bytes 2949124
  298.3 41.5 %collective-permute-start.1 = (bf16[3,128,1280]{2,1,0:T(8,128)(2,1)}, bf16[3,128,1280]{2,1,0:T(8,128)(2,1)}, u32[]{:S(2)}, u32[]{:S(2)}) collective-permute-start(bf16[3,128,1280]{2,1,0:T(8,128)(2,1)} %get-tuple-element.67.refs_0_), channel_id=1, source_target_pairs={{0,4},{1,3},{2,6},{3,1},{4,0},{5,7},{6,2},{7,5}} | collective-permute-start | bytes 2949128 | tf_op jit(solution)/shard_map/ppermute | solution.py:504
  317.2 30.9 %collective-permute-start.16 = (bf16[3,128,1280]{2,1,0:T(8,128)(2,1)S(1)}, bf16[3,128,1280]{2,1,0:T(8,128)(2,1)S(1)}, u32[]{:S(2)}, u32[]{:S(2)}) collective-permute-start(bf16[3,128,1280]{2,1,0:T(8,128)(2,1)S(1)} %collective-permute-done.14.refs_1_), channel_id=1, source_target_pairs={{0,4},{1,3},{2,6},{3,1},{4,0},{5,7},{6,2},{7,5}} | collective-permute-start | bytes 2949128 | tf_op jit(solution)/shard_map/ppermute | solution.py:504
  318.6 30.5 %collective-permute-start.18 = (bf16[3,128,1280]{2,1,0:T(8,128)(2,1)S(1)}, bf16[3,128,1280]{2,1,0:T(8,128)(2,1)S(1)}, u32[]{:S(2)}, u32[]{:S(2)}) collective-permute-start(bf16[3,128,1280]{2,1,0:T(8,128)(2,1)S(1)} %collective-permute-done.14.refs_1_), channel_id=1, source_target_pairs={{0,1},{1,0},{2,3},{3,2},{4,5},{5,4},{6,7},{7,6}} | collective-permute-start | bytes 2949128 | tf_op jit(solution)/shard_map/ppermute | solution.py:504
  318.6 31.4 %collective-permute-start.19 = (bf16[3,128,1280]{2,1,0:T(8,128)(2,1)S(1)}, bf16[3,128,1280]{2,1,0:T(8,128)(2,1)S(1)}, u32[]{:S(2)}, u32[]{:S(2)}) collective-permute-start(bf16[3,128,1280]{2,1,0:T(8,128)(2,1)S(1)} %collective-permute-done.15.refs_2_), channel_id=1, source_target_pairs={{0,1},{1,0},{2,3},{3,2},{4,5},{5,4},{6,7},{7,6}} | collective-permute-start | bytes 2949128 | tf_op jit(solution)/shard_map/ppermute | solution.py:504
  338.4 20.4 %collective-permute-start.9 = (bf16[3,128,1280]{2,1,0:T(8,128)(2,1)S(1)}, bf16[3,128,1280]{2,1,0:T(8,128)(2,1)}, u32[]{:S(2)}, u32[]{:S(2)}) collective-permute-start(bf16[3,128,1280]{2,1,0:T(8,128)(2,1)S(1)} %collective-permute-done.7.refs_1_), channel_id=1, source_target_pairs={{0,4},{1,3},{2,6},{3,1},{4,0},{5,7},{6,2},{7,5}} | collective-permute-start | bytes 2949128 | tf_op jit(solution)/shard_map/ppermute | solution.py:504
  339.8 19.9 %collective-permute-start.11 = (bf16[3,128,1280]{2,1,0:T(8,128)(2,1)S(1)}, bf16[3,128,1280]{2,1,0:T(8,128)(2,1)S(1)}, u32[]{:S(2)}, u32[]{:S(2)}) collective-permute-start(bf16[3,128,1280]{2,1,0:T(8,128)(2,1)S(1)} %collective-permute-done.7.refs_1_), channel_id=1, source_target_pairs={{0,1},{1,0},{2,3},{3,2},{4,5},{5,4},{6,7},{7,6}} | collective-permute-start | bytes 2949128 | tf_op jit(solution)/shard_map/ppermute | solution.py:504
  348.1 11.6 %collective-permute-start.12 = (bf16[3,128,1280]{2,1,0:T(8,128)(2,1)S(1)}, bf16[3,128,1280]{2,1,0:T(8,128)(2,1)S(1)}, u32[]{:S(2)}, u32[]{:S(2)}) collective-permute-start(bf16[3,128,1280]{2,1,0:T(8,128)(2,1)S(1)} %collective-permute-done.8.refs_2_), channel_id=1, source_target_pairs={{0,1},{1,0},{2,3},{3,2},{4,5},{5,4},{6,7},{7,6}} | collective-permute-start | bytes 2949128 | tf_op jit(solution)/shard_map/ppermute | solution.py:504
  349.2 20.1 %collective-permute-start.2 = (bf16[3,128,1280]{2,1,0:T(8,128)(2,1)}, bf16[3,128,1280]{2,1,0:T(8,128)(2,1)}, u32[]{:S(2)}, u32[]{:S(2)}) collective-permute-start(bf16[3,128,1280]{2,1,0:T(8,128)(2,1)} %collective-permute-done.refs_1_), channel_id=1, source_target_pairs={{0,4},{1,3},{2,6},{3,1},{4,0},{5,7},{6,2},{7,5}} | collective-permute-start | bytes 2949128 | tf_op jit(solution)/shard_map/ppermute | solution.py:504
  350.1 19.9 %collective-permute-start.20 = (bf16[3,128,1280]{2,1,0:T(8,128)(2,1)S(1)}, bf16[3,128,1280]{2,1,0:T(8,128)(2,1)S(1)}, u32[]{:S(2)}, u32[]{:S(2)}) collective-permute-start(bf16[3,128,1280]{2,1,0:T(8,128)(2,1)S(1)} %collective-permute-done.16.refs_3_), channel_id=1, source_target_pairs={{0,1},{1,0},{2,3},{3,2},{4,5},{5,4},{6,7},{7,6}} | collective-permute-start | bytes 2949128 | tf_op jit(solution)/shard_map/ppermute | solution.py:504
  358.7 74.5 %collective-permute-start.13 = (bf16[3,128,1280]{2,1,0:T(8,128)(2,1)}, bf16[3,128,1280]{2,1,0:T(8,128)(2,1)}, u32[]{:S(2)}, u32[]{:S(2)}) collective-permute-start(bf16[3,128,1280]{2,1,0:T(8,128)(2,1)} %collective-permute-done.9.refs_3_), channel_id=1, source_target_pairs={{0,1},{1,0},{2,3},{3,2},{4,5},{5,4},{6,7},{7,6}} | collective-permute-start | bytes 2949128 | tf_op jit(solution)/shard_map/ppermute | solution.py:504
  359.7 102.2 %collective-permute-start.3 = (bf16[3,128,1280]{2,1,0:T(8,128)(2,1)}, bf16[3,128,1280]{2,1,0:T(8,128)(2,1)}, u32[]{:S(2)}, u32[]{:S(2)}) collective-permute-start(bf16[3,128,1280]{2,1,0:T(8,128)(2,1)} %get-tuple-element.67.refs_0_), channel_id=1, source_target_pairs={{0,1},{1,0},{2,3},{3,2},{4,5},{5,4},{6,7},{7,6}} | collective-permute-start | bytes 2949128 | tf_op jit(solution)/shard_map/ppermute | solution.py:504
  359.8 102.1 %collective-permute-start.4 = (bf16[3,128,1280]{2,1,0:T(8,128)(2,1)}, bf16[3,128,1280]{2,1,0:T(8,128)(2,1)}, u32[]{:S(2)}, u32[]{:S(2)}) collective-permute-start(bf16[3,128,1280]{2,1,0:T(8,128)(2,1)} %collective-permute-done.refs_1_), channel_id=1, source_target_pairs={{0,1},{1,0},{2,3},{3,2},{4,5},{5,4},{6,7},{7,6}} | collective-permute-start | bytes 2949128 | tf_op jit(solution)/shard_map/ppermute | solution.py:504
  369.2 92.6 %collective-permute-start.5 = (bf16[3,128,1280]{2,1,0:T(8,128)(2,1)}, bf16[3,128,1280]{2,1,0:T(8,128)(2,1)}, u32[]{:S(2)}, u32[]{:S(2)}) collective-permute-start(bf16[3,128,1280]{2,1,0:T(8,128)(2,1)} %collective-permute-done.1.refs_2_), channel_id=1, source_target_pairs={{0,1},{1,0},{2,3},{3,2},{4,5},{5,4},{6,7},{7,6}} | collective-permute-start | bytes 2949128 | tf_op jit(solution)/shard_map/ppermute | solution.py:504
  369.9 91.9 %collective-permute-start.6 = (bf16[3,128,1280]{2,1,0:T(8,128)(2,1)}, bf16[3,128,1280]{2,1,0:T(8,128)(2,1)}, u32[]{:S(2)}, u32[]{:S(2)}) collective-permute-start(bf16[3,128,1280]{2,1,0:T(8,128)(2,1)} %collective-permute-done.2.refs_3_), channel_id=1, source_target_pairs={{0,1},{1,0},{2,3},{3,2},{4,5},{5,4},{6,7},{7,6}} | collective-permute-start | bytes 2949128 | tf_op jit(solution)/shard_map/ppermute | solution.py:504
  (9 other events, 188.9 us)

commit v4 on v3

--- a/solution.py
+++ b/solution.py
@@ -150,7 +150,7 @@
     mid = n // 2
     turn, low = n, n + 1
     end = low + n
-    steps = end + 7
+    steps = end + 6
 
     def kernel(*refs):
         refs = list(refs)
@@ -244,7 +244,7 @@
                 c.wait()
 
         def finish(out, number):
-            t = j - (4 if number < 2 else 6)
+            t = j - (4 if number < 2 else 5)
             far_copy(t).wait()
             for i in range(3):
                 done = both(stay2[t % 2, i], recv2[t % 5, i])
@@ -257,7 +257,7 @@
 
         for number, first in enumerate((0, mid, low, low + mid)):
 
-            @pl.when(between(first + (4 if number < 2 else 6), mid))
+            @pl.when(between(first + (4 if number < 2 else 5), mid))
             def _(number=number):
                 finish(owns[number], number)
 
@@ -419,7 +419,7 @@
     def shard(first):
         return pl.BlockSpec((3, BLK, FT), lambda j: (0, 0, jnp.clip(j - first, 0, mid - 1))), shaped((3, BLK, WIDE))
 
-    outs = [shard(first) for first in (4, 4 + mid, low + 6, low + 6 + mid)]
+    outs = [shard(first) for first in (4, 4 + mid, low + 5, low + 5 + mid)]
     outs += [(whole, shaped((3, 3, BLK, WIDE))), (whole, shaped((4, 3, BLK, WIDE))), (pl.BlockSpec((8, 128), lambda j: (0, 0)), shaped((8, 128), F32))]
     sem = pltpu.SemaphoreType.DMA
     quarter = lambda *lead: pltpu.VMEM((*lead, 3, BLK, FT), BF16)

time: 491 us -> 495 us (level)
  Pallas kernels: 390 us -> 395 us
  transfers between devices with their start and end apart: 21 -> 21, of which waited for: 7 -> 8; matrix products, arithmetic and copies ran while one was open for 0% -> 0% of each run, Pallas kernels for 19% -> 18%
where the time goes in v4:
time: 495 us
  Pallas kernels  395 us (80%)
  waiting for transfers between devices  85.9 us (17%)
  starting transfers between devices  12.6 us (3%)
    pallas_call x1, Pallas kernels, backward(): pl.pallas_call(kernel, grid_spec=pltpu.PrefetchScalarGridSpec(num_scalar_...  228 us
    pallas_call x5, Pallas kernels, adamw(): call(kernel, (8, steps), ins, outs, [pltpu.VMEM((3, BLK, ft), BF16)], flo...  119 us
    ppermute x21, waiting for transfers between devices, swap(): return lax.ppermute(a, 'dp', STAGES[stage])  85.9 us
    pallas_call x1, Pallas kernels, forward(): call(kernel, (n + T // SUB,), [pl.BlockSpec((T, D), lambda j, m: (0, 0),...  47.6 us
    ppermute x21, starting transfers between devices, swap(): return lax.ppermute(a, 'dp', STAGES[stage])  12.6 us
  transfers between devices with their start and end apart: 21, of which 8 were waited for; matrix products, arithmetic and copies ran while one was open for 0% of the time, Pallas kernels for 18%

profile of v4, /device:TPU:0, one launch (start us, length us, event | category | flops | bytes accessed | tf_op | source)
XLA Modules:
  0.0 495.1 jit_solution(11822493201577604013)
XLA Ops:
  0.6 47.6 %shard_map.178 = (f32[2048,2560]{1,0:T(8,128)}, f32[2048,2560]{1,0:T(8,128)}, bf16[2048,1024]{1,0:T(8,128)(2,1)}, bf16[2048,1024]{1,0:T(8,128)(2,1)}, bf16[1024,...) custom-call(s32[1]{0:T(128)} %bitcast.me_ref, bf16[2048,1024]{1,0:T(8,128)(2,1)} %bitcast.3, ...), custom_call_target="tpu_custom_call" | custom-call | flops 32212254720 | bytes 90000000 | tf_op jit(solution)/shard_map/pallas_call | solution.py:125
  48.3 227.7 %backward.1 = (bf16[3,128,1280]{2,1,0:T(8,128)(2,1)}, bf16[3,128,1280]{2,1,0:T(8,128)(2,1)}, bf16[3,128,1280]{2,1,0:T(8,128)(2,1)}, bf16[3,128,1280]{2,1,0:T(8,1...) custom-call(bf16[2048,1024]{1,0:T(8,128)(2,1)} %bitcast.5, ...), custom_call_target="tpu_custom_call" | custom-call | flops 128849018880 | bytes 120000000 | tf_op jit(solution)/shard_map/backward/pallas_call | solution.py:431
  276.0 1.6 collective-permute-start.14
  278.1 1.0 collective-permute-start.7
  279.1 0.9 collective-permute-start.8
  280.1 20.8 %collective-permute-done.14.refs_1_ = bf16[3,128,1280]{2,1,0:T(8,128)(2,1)S(1)} collective-permute-done((bf16[3,128,1280]{2,1,0:T(8,128)(2,1)}, bf16[3,128,1280]{2,1,0:T(8,128)(2,1)S(1)}, u32[]{:S(2)}, u32[]{:S(2)}) %collective-permute-start.14) | collective-permute-done | bytes 983072 | tf_op jit(solution)/shard_map/ppermute | solution.py:504
  300.8 1.6 collective-permute-done.15.refs_2_
  302.9 1.1 collective-permute-start.1
  304.0 17.9 %collective-permute-done.7.refs_1_ = bf16[3,128,1280]{2,1,0:T(8,128)(2,1)S(1)} collective-permute-done((bf16[3,128,1280]{2,1,0:T(8,128)(2,1)}, bf16[3,128,1280]{2,1,0:T(8,128)(2,1)S(1)}, u32[]{:S(2)}, u32[]{:S(2)}) %collective-permute-start.7) | collective-permute-done | bytes 983072 | tf_op jit(solution)/shard_map/ppermute | solution.py:504
  321.9 1.1 collective-permute-start.16
  324.0 19.1 %collective-permute-done.refs_1_ = bf16[3,128,1280]{2,1,0:T(8,128)(2,1)} collective-permute-done((bf16[3,128,1280]{2,1,0:T(8,128)(2,1)}, bf16[3,128,1280]{2,1,0:T(8,128)(2,1)}, u32[]{:S(2)}, u32[]{:S(2)}) %collective-permute-start) | collective-permute-done | bytes 983072 | tf_op jit(solution)/shard_map/ppermute | solution.py:504
  343.1 1.1 collective-permute-start.9
  344.2 8.4 %collective-permute-done.16.refs_3_ = bf16[3,128,1280]{2,1,0:T(8,128)(2,1)S(1)} collective-permute-done((bf16[3,128,1280]{2,1,0:T(8,128)(2,1)S(1)}, bf16[3,128,1280]{2,1,0:T(8,128)(2,1)S(1)}, u32[]{:S(2)}, u32[]{:S(2)}) %collective-permute-start.16) | collective-permute-done | bytes 983072 | tf_op jit(solution)/shard_map/ppermute | solution.py:504
  352.7 1.1 collective-permute-start.12
  353.7 0.9 collective-permute-start.2
  354.6 8.7 %collective-permute-done.9.refs_3_ = bf16[3,128,1280]{2,1,0:T(8,128)(2,1)} collective-permute-done((bf16[3,128,1280]{2,1,0:T(8,128)(2,1)S(1)}, bf16[3,128,1280]{2,1,0:T(8,128)(2,1)}, u32[]{:S(2)}, u32[]{:S(2)}) %collective-permute-start.9) | collective-permute-done | bytes 983072 | tf_op jit(solution)/shard_map/ppermute | solution.py:504
  363.3 1.0 collective-permute-start.13
  364.8 9.0 %collective-permute-done.2.refs_3_ = bf16[3,128,1280]{2,1,0:T(8,128)(2,1)} collective-permute-done((bf16[3,128,1280]{2,1,0:T(8,128)(2,1)}, bf16[3,128,1280]{2,1,0:T(8,128)(2,1)}, u32[]{:S(2)}, u32[]{:S(2)}) %collective-permute-start.2) | collective-permute-done | bytes 983072 | tf_op jit(solution)/shard_map/ppermute | solution.py:504
  374.6 0.9 copy-done.11
  375.5 16.9 %shard_map.179 = (bf16[2,1024,2560]{2,1,0:T(8,128)(2,1)}, bf16[2,1024,2560]{2,1,0:T(8,128)(2,1)}, bf16[2,2560,1024]{2,1,0:T(8,128)(2,1)}, f32[2,1024,2560]{2,1,0...) custom-call(s32[1]{0:T(128)} %bitcast.me_ref, ...), custom_call_target="tpu_custom_call" | custom-call | flops 393216000 | bytes 43253760 | tf_op jit(solution)/shard_map/pallas_call | solution.py:492
  392.3 17.0 %shard_map.180 = (bf16[2,1024,2560]{2,1,0:T(8,128)(2,1)}, bf16[2,1024,2560]{2,1,0:T(8,128)(2,1)}, bf16[2,2560,1024]{2,1,0:T(8,128)(2,1)}, f32[2,1024,2560]{2,1,0...) custom-call(s32[1]{0:T(128)} %bitcast.me_ref, ...), custom_call_target="tpu_custom_call", output_to_operand_aliasing={{0}: (19, {}), {1}: (20, {}), {2}: (21, {}), {3}: (22, {}),... | custom-call | flops 393216000 | bytes 43253760 | tf_op jit(solution)/shard_map/pallas_call | solution.py:492
  409.4 28.4 %shard_map.181 = (bf16[2,1024,2560]{2,1,0:T(8,128)(2,1)}, bf16[2,1024,2560]{2,1,0:T(8,128)(2,1)}, bf16[2,2560,1024]{2,1,0:T(8,128)(2,1)}, f32[2,1024,2560]{2,1,0...) custom-call(s32[1]{0:T(128)} %bitcast.me_ref, ...), custom_call_target="tpu_custom_call", output_to_operand_aliasing={{0}: (19, {}), {1}: (20, {}), {2}: (21, {}), {3}: (22, {}),... | custom-call | flops 786432000 | bytes 86507520 | tf_op jit(solution)/shard_map/pallas_call | solution.py:492
  437.8 28.6 %shard_map.182 = (bf16[2,1024,2560]{2,1,0:T(8,128)(2,1)}, bf16[2,1024,2560]{2,1,0:T(8,128)(2,1)}, bf16[2,2560,1024]{2,1,0:T(8,128)(2,1)}, f32[2,1024,2560]{2,1,0...) custom-call(s32[1]{0:T(128)} %bitcast.me_ref, ...), custom_call_target="tpu_custom_call", output_to_operand_aliasing={{0}: (19, {}), {1}: (20, {}), {2}: (21, {}), {3}: (22, {}),... | custom-call | flops 786432000 | bytes 86507520 | tf_op jit(solution)/shard_map/pallas_call | solution.py:492
  466.5 28.4 %shard_map.183 = (bf16[2,1024,2560]{2,1,0:T(8,128)(2,1)}, bf16[2,1024,2560]{2,1,0:T(8,128)(2,1)}, bf16[2,2560,1024]{2,1,0:T(8,128)(2,1)}, f32[2,1024,2560]{2,1,0...) custom-call(s32[1]{0:T(128)} %bitcast.me_ref, ...), custom_call_target="tpu_custom_call", output_to_operand_aliasing={{0}: (19, {}), {1}: (20, {}), {2}: (21, {}), {3}: (22, {}),... | custom-call | flops 786432000 | bytes 86507520 | tf_op jit(solution)/shard_map/pallas_call | solution.py:492
  (49 shorter events, 3.3 us)
Async XLA Ops:
  276.0 24.9 %collective-permute-start.14 = (bf16[3,128,1280]{2,1,0:T(8,128)(2,1)}, bf16[3,128,1280]{2,1,0:T(8,128)(2,1)S(1)}, u32[]{:S(2)}, u32[]{:S(2)}) collective-permute-start(bf16[3,128,1280]{2,1,0:T(8,128)(2,1)} %get-tuple-element.69.refs_0_), channel_id=1, source_target_pairs={{0,2},{1,5},{2,0},{3,7},{4,6},{5,1},{6,4},{7,3}} | collective-permute-start | bytes 2949128 | tf_op jit(solution)/shard_map/ppermute | solution.py:504
  277.6 24.8 %collective-permute-start.15 = (bf16[3,128,1280]{2,1,0:T(8,128)(2,1)}, bf16[3,128,1280]{2,1,0:T(8,128)(2,1)S(1)}, u32[]{:S(2)}, u32[]{:S(2)}) collective-permute-start(bf16[3,128,1280]{2,1,0:T(8,128)(2,1)} %get-tuple-element.69.refs_0_), channel_id=1, source_target_pairs={{0,4},{1,3},{2,6},{3,1},{4,0},{5,7},{6,2},{7,5}} | collective-permute-start | bytes 2949128 | tf_op jit(solution)/shard_map/ppermute | solution.py:504
  278.1 24.8 %collective-permute-start.17 = (bf16[3,128,1280]{2,1,0:T(8,128)(2,1)}, bf16[3,128,1280]{2,1,0:T(8,128)(2,1)S(1)}, u32[]{:S(2)}, u32[]{:S(2)}) collective-permute-start(bf16[3,128,1280]{2,1,0:T(8,128)(2,1)} %get-tuple-element.69.refs_0_), channel_id=1, source_target_pairs={{0,1},{1,0},{2,3},{3,2},{4,5},{5,4},{6,7},{7,6}} | collective-permute-start | bytes 2949128 | tf_op jit(solution)/shard_map/ppermute | solution.py:504
  278.1 43.8 %collective-permute-start.7 = (bf16[3,128,1280]{2,1,0:T(8,128)(2,1)}, bf16[3,128,1280]{2,1,0:T(8,128)(2,1)S(1)}, u32[]{:S(2)}, u32[]{:S(2)}) collective-permute-start(bf16[3,128,1280]{2,1,0:T(8,128)(2,1)} %get-tuple-element.68.refs_0_), channel_id=1, source_target_pairs={{0,2},{1,5},{2,0},{3,7},{4,6},{5,1},{6,4},{7,3}} | collective-permute-start | bytes 2949128 | tf_op jit(solution)/shard_map/ppermute | solution.py:504
  279.1 44.3 %collective-permute-start.8 = (bf16[3,128,1280]{2,1,0:T(8,128)(2,1)}, bf16[3,128,1280]{2,1,0:T(8,128)(2,1)S(1)}, u32[]{:S(2)}, u32[]{:S(2)}) collective-permute-start(bf16[3,128,1280]{2,1,0:T(8,128)(2,1)} %get-tuple-element.68.refs_0_), channel_id=1, source_target_pairs={{0,4},{1,3},{2,6},{3,1},{4,0},{5,7},{6,2},{7,5}} | collective-permute-start | bytes 2949128 | tf_op jit(solution)/shard_map/ppermute | solution.py:504
  300.8 91.5 %copy-start.3 = (bf16[3,128,1280]{2,1,0:T(8,128)(2,1)}, bf16[3,128,1280]{2,1,0:T(8,128)(2,1)S(1)}, u32[]{:S(2)}) copy-start(bf16[3,128,1280]{2,1,0:T(8,128)(2,1)S(1)} %collective-permute-done.14.refs_1_) | copy-start | bytes 2949124
  300.8 22.6 %collective-permute-start.10 = (bf16[3,128,1280]{2,1,0:T(8,128)(2,1)}, bf16[3,128,1280]{2,1,0:T(8,128)(2,1)S(1)}, u32[]{:S(2)}, u32[]{:S(2)}) collective-permute-start(bf16[3,128,1280]{2,1,0:T(8,128)(2,1)} %get-tuple-element.68.refs_0_), channel_id=1, source_target_pairs={{0,1},{1,0},{2,3},{3,2},{4,5},{5,4},{6,7},{7,6}} | collective-permute-start | bytes 2949128 | tf_op jit(solution)/shard_map/ppermute | solution.py:504
  302.4 62.4 %copy-start.4 = (bf16[3,128,1280]{2,1,0:T(8,128)(2,1)}, bf16[3,128,1280]{2,1,0:T(8,128)(2,1)S(1)}, u32[]{:S(2)}) copy-start(bf16[3,128,1280]{2,1,0:T(8,128)(2,1)S(1)} %collective-permute-done.15.refs_2_) | copy-start | bytes 2949124
  302.4 40.7 %collective-permute-start = (bf16[3,128,1280]{2,1,0:T(8,128)(2,1)}, bf16[3,128,1280]{2,1,0:T(8,128)(2,1)}, u32[]{:S(2)}, u32[]{:S(2)}) collective-permute-start(bf16[3,128,1280]{2,1,0:T(8,128)(2,1)} %get-tuple-element.67.refs_0_), channel_id=1, source_target_pairs={{0,2},{1,5},{2,0},{3,7},{4,6},{5,1},{6,4},{7,3}} | collective-permute-start | bytes 2949128 | tf_op jit(solution)/shard_map/ppermute | solution.py:504
  302.9 71.0 %copy-start.5 = (bf16[3,128,1280]{2,1,0:T(8,128)(2,1)}, bf16[3,128,1280]{2,1,0:T(8,128)(2,1)S(1)}, u32[]{:S(2)}) copy-start(bf16[3,128,1280]{2,1,0:T(8,128)(2,1)S(1)} %collective-permute-done.17.refs_4_) | copy-start | bytes 2949124
  302.9 41.3 %collective-permute-start.1 = (bf16[3,128,1280]{2,1,0:T(8,128)(2,1)}, bf16[3,128,1280]{2,1,0:T(8,128)(2,1)}, u32[]{:S(2)}, u32[]{:S(2)}) collective-permute-start(bf16[3,128,1280]{2,1,0:T(8,128)(2,1)} %get-tuple-element.67.refs_0_), channel_id=1, source_target_pairs={{0,4},{1,3},{2,6},{3,1},{4,0},{5,7},{6,2},{7,5}} | collective-permute-start | bytes 2949128 | tf_op jit(solution)/shard_map/ppermute | solution.py:504
  321.9 30.7 %collective-permute-start.16 = (bf16[3,128,1280]{2,1,0:T(8,128)(2,1)S(1)}, bf16[3,128,1280]{2,1,0:T(8,128)(2,1)S(1)}, u32[]{:S(2)}, u32[]{:S(2)}) collective-permute-start(bf16[3,128,1280]{2,1,0:T(8,128)(2,1)S(1)} %collective-permute-done.14.refs_1_), channel_id=1, source_target_pairs={{0,4},{1,3},{2,6},{3,1},{4,0},{5,7},{6,2},{7,5}} | collective-permute-start | bytes 2949128 | tf_op jit(solution)/shard_map/ppermute | solution.py:504
  323.5 30.3 %collective-permute-start.18 = (bf16[3,128,1280]{2,1,0:T(8,128)(2,1)S(1)}, bf16[3,128,1280]{2,1,0:T(8,128)(2,1)S(1)}, u32[]{:S(2)}, u32[]{:S(2)}) collective-permute-start(bf16[3,128,1280]{2,1,0:T(8,128)(2,1)S(1)} %collective-permute-done.14.refs_1_), channel_id=1, source_target_pairs={{0,1},{1,0},{2,3},{3,2},{4,5},{5,4},{6,7},{7,6}} | collective-permute-start | bytes 2949128 | tf_op jit(solution)/shard_map/ppermute | solution.py:504
  323.5 31.1 %collective-permute-start.19 = (bf16[3,128,1280]{2,1,0:T(8,128)(2,1)S(1)}, bf16[3,128,1280]{2,1,0:T(8,128)(2,1)S(1)}, u32[]{:S(2)}, u32[]{:S(2)}) collective-permute-start(bf16[3,128,1280]{2,1,0:T(8,128)(2,1)S(1)} %collective-permute-done.15.refs_2_), channel_id=1, source_target_pairs={{0,1},{1,0},{2,3},{3,2},{4,5},{5,4},{6,7},{7,6}} | collective-permute-start | bytes 2949128 | tf_op jit(solution)/shard_map/ppermute | solution.py:504
  343.1 20.2 %collective-permute-start.9 = (bf16[3,128,1280]{2,1,0:T(8,128)(2,1)S(1)}, bf16[3,128,1280]{2,1,0:T(8,128)(2,1)}, u32[]{:S(2)}, u32[]{:S(2)}) collective-permute-start(bf16[3,128,1280]{2,1,0:T(8,128)(2,1)S(1)} %collective-permute-done.7.refs_1_), channel_id=1, source_target_pairs={{0,4},{1,3},{2,6},{3,1},{4,0},{5,7},{6,2},{7,5}} | collective-permute-start | bytes 2949128 | tf_op jit(solution)/shard_map/ppermute | solution.py:504
  344.2 20.1 %collective-permute-start.11 = (bf16[3,128,1280]{2,1,0:T(8,128)(2,1)S(1)}, bf16[3,128,1280]{2,1,0:T(8,128)(2,1)S(1)}, u32[]{:S(2)}, u32[]{:S(2)}) collective-permute-start(bf16[3,128,1280]{2,1,0:T(8,128)(2,1)S(1)} %collective-permute-done.7.refs_1_), channel_id=1, source_target_pairs={{0,1},{1,0},{2,3},{3,2},{4,5},{5,4},{6,7},{7,6}} | collective-permute-start | bytes 2949128 | tf_op jit(solution)/shard_map/ppermute | solution.py:504
  352.7 11.6 %collective-permute-start.12 = (bf16[3,128,1280]{2,1,0:T(8,128)(2,1)S(1)}, bf16[3,128,1280]{2,1,0:T(8,128)(2,1)S(1)}, u32[]{:S(2)}, u32[]{:S(2)}) collective-permute-start(bf16[3,128,1280]{2,1,0:T(8,128)(2,1)S(1)} %collective-permute-done.8.refs_2_), channel_id=1, source_target_pairs={{0,1},{1,0},{2,3},{3,2},{4,5},{5,4},{6,7},{7,6}} | collective-permute-start | bytes 2949128 | tf_op jit(solution)/shard_map/ppermute | solution.py:504
  353.7 20.1 %collective-permute-start.2 = (bf16[3,128,1280]{2,1,0:T(8,128)(2,1)}, bf16[3,128,1280]{2,1,0:T(8,128)(2,1)}, u32[]{:S(2)}, u32[]{:S(2)}) collective-permute-start(bf16[3,128,1280]{2,1,0:T(8,128)(2,1)} %collective-permute-done.refs_1_), channel_id=1, source_target_pairs={{0,4},{1,3},{2,6},{3,1},{4,0},{5,7},{6,2},{7,5}} | collective-permute-start | bytes 2949128 | tf_op jit(solution)/shard_map/ppermute | solution.py:504
  354.6 19.9 %collective-permute-start.20 = (bf16[3,128,1280]{2,1,0:T(8,128)(2,1)S(1)}, bf16[3,128,1280]{2,1,0:T(8,128)(2,1)S(1)}, u32[]{:S(2)}, u32[]{:S(2)}) collective-permute-start(bf16[3,128,1280]{2,1,0:T(8,128)(2,1)S(1)} %collective-permute-done.16.refs_3_), channel_id=1, source_target_pairs={{0,1},{1,0},{2,3},{3,2},{4,5},{5,4},{6,7},{7,6}} | collective-permute-start | bytes 2949128 | tf_op jit(solution)/shard_map/ppermute | solution.py:504
  363.3 74.5 %collective-permute-start.13 = (bf16[3,128,1280]{2,1,0:T(8,128)(2,1)}, bf16[3,128,1280]{2,1,0:T(8,128)(2,1)}, u32[]{:S(2)}, u32[]{:S(2)}) collective-permute-start(bf16[3,128,1280]{2,1,0:T(8,128)(2,1)} %collective-permute-done.9.refs_3_), channel_id=1, source_target_pairs={{0,1},{1,0},{2,3},{3,2},{4,5},{5,4},{6,7},{7,6}} | collective-permute-start | bytes 2949128 | tf_op jit(solution)/shard_map/ppermute | solution.py:504
  364.3 102.2 %collective-permute-start.3 = (bf16[3,128,1280]{2,1,0:T(8,128)(2,1)}, bf16[3,128,1280]{2,1,0:T(8,128)(2,1)}, u32[]{:S(2)}, u32[]{:S(2)}) collective-permute-start(bf16[3,128,1280]{2,1,0:T(8,128)(2,1)} %get-tuple-element.67.refs_0_), channel_id=1, source_target_pairs={{0,1},{1,0},{2,3},{3,2},{4,5},{5,4},{6,7},{7,6}} | collective-permute-start | bytes 2949128 | tf_op jit(solution)/shard_map/ppermute | solution.py:504
  364.3 102.1 %collective-permute-start.4 = (bf16[3,128,1280]{2,1,0:T(8,128)(2,1)}, bf16[3,128,1280]{2,1,0:T(8,128)(2,1)}, u32[]{:S(2)}, u32[]{:S(2)}) collective-permute-start(bf16[3,128,1280]{2,1,0:T(8,128)(2,1)} %collective-permute-done.refs_1_), channel_id=1, source_target_pairs={{0,1},{1,0},{2,3},{3,2},{4,5},{5,4},{6,7},{7,6}} | collective-permute-start | bytes 2949128 | tf_op jit(solution)/shard_map/ppermute | solution.py:504
  373.8 92.6 %collective-permute-start.5 = (bf16[3,128,1280]{2,1,0:T(8,128)(2,1)}, bf16[3,128,1280]{2,1,0:T(8,128)(2,1)}, u32[]{:S(2)}, u32[]{:S(2)}) collective-permute-start(bf16[3,128,1280]{2,1,0:T(8,128)(2,1)} %collective-permute-done.1.refs_2_), channel_id=1, source_target_pairs={{0,1},{1,0},{2,3},{3,2},{4,5},{5,4},{6,7},{7,6}} | collective-permute-start | bytes 2949128 | tf_op jit(solution)/shard_map/ppermute | solution.py:504
  374.5 91.9 %collective-permute-start.6 = (bf16[3,128,1280]{2,1,0:T(8,128)(2,1)}, bf16[3,128,1280]{2,1,0:T(8,128)(2,1)}, u32[]{:S(2)}, u32[]{:S(2)}) collective-permute-start(bf16[3,128,1280]{2,1,0:T(8,128)(2,1)} %collective-permute-done.2.refs_3_), channel_id=1, source_target_pairs={{0,1},{1,0},{2,3},{3,2},{4,5},{5,4},{6,7},{7,6}} | collective-permute-start | bytes 2949128 | tf_op jit(solution)/shard_map/ppermute | solution.py:504
  (9 other events, 188.0 us)
